TPU v7x, 32 devices: a whole 2x2x4 slice. The times are simulated.
32 devices in a mesh: seq: 16 (over z, x, core), head: 2 (over y).
Axes of the slice: x: 2, y: 2, z: 4, core: 2. Of those that a mesh axis runs over, the one named last changes fastest.
Arguments:
- activations: bfloat16 [4096, 4096], P('seq', 'head'), may hold values from -6 to 6
- grad_out: bfloat16 [4096, 4096], P('seq', 'head'), may hold values from -0.03125 to 0.03125
- query_weight: bfloat16 [4096, 4096], P('seq', 'head'), may hold values from -0.09375 to 0.09375
- key_weight: bfloat16 [4096, 1024], P('seq', 'head'), may hold values from -0.09375 to 0.09375
- value_weight: bfloat16 [4096, 1024], P('seq', 'head'), may hold values from -0.09375 to 0.09375
Outputs:
- grad_input: bfloat16 [4096, 4096], P('seq', 'head')
All inputs are finite; a program needn't handle non-finite values.
Results may differ from a plain program's by a relative error of at most 0.018.
Values may be sent and summed in bfloat16 or wider, within the bound.
No kernel may reach another device: no remote copies, remote signals or barrier semaphores. Data moves between devices by JAX's collectives and lax.ppermute only.
A program may use at most 128 MiB of HBM per device.

v0:
```python
import jax
import jax.numpy as jnp
from jax import lax
from jax.sharding import PartitionSpec as P

HEADS = 32
KV_HEADS = 8
HEAD_DIM = 128


def contract_rows(grads, weight):
    return lax.dot_general(
        grads, weight, (((1,), (1,)), ((), ())), preferred_element_type=jnp.float32
    )


def local(activations, grad_out, query_weight, key_weight, value_weight):
    factor = HEAD_DIM ** (-0.5)
    group_size = HEADS // KV_HEADS
    gathered = (
        lax.all_gather(query_weight, "seq", axis=0, tiled=True),
        lax.all_gather(key_weight, "seq", axis=0, tiled=True),
        lax.all_gather(value_weight, "seq", axis=0, tiled=True),
    )
    query_full, key_full, value_full = gathered
    tokens_dev = activations.shape[0]
    portion = lax.all_gather(activations, "head", axis=1, tiled=True)
    projected = tuple(
        (jnp.dot(portion, weight, preferred_element_type=jnp.float32) for weight in gathered)
    )
    queries, key_rows, value_rows = tuple((item.astype(jnp.bfloat16) for item in projected))
    kv_groups = key_full.shape[1] // HEAD_DIM
    query_heads = queries.reshape(tokens_dev, kv_groups, group_size, HEAD_DIM)
    key_heads = key_rows.reshape(tokens_dev, kv_groups, HEAD_DIM)
    value_heads = value_rows.reshape(tokens_dev, kv_groups, HEAD_DIM)
    grad_heads = grad_out.reshape(tokens_dev, kv_groups, group_size, HEAD_DIM)
    kv_state = jnp.einsum(
        "tgd,tge->gde", key_heads, value_heads, preferred_element_type=jnp.float32
    ).astype(jnp.bfloat16)
    grad_state = (
        factor
        * jnp.einsum("tghd,tghe->gde", query_heads, grad_heads, preferred_element_type=jnp.float32)
    ).astype(jnp.bfloat16)
    every_kv, every_grad = (
        lax.all_gather(kv_state[None], "seq", axis=0, tiled=True),
        lax.all_gather(grad_state[None], "seq", axis=0, tiled=True),
    )
    position = lax.axis_index("seq")
    order = jnp.arange(every_kv.shape[0], dtype=jnp.int32)
    before = (order < position).astype(jnp.bfloat16)
    after = (order > position).astype(jnp.bfloat16)
    prefix = jnp.einsum("n,ngde->gde", before, every_kv, preferred_element_type=jnp.float32)
    suffix = jnp.einsum("n,ngde->gde", after, every_grad, preferred_element_type=jnp.float32)
    prefix_half = prefix.astype(jnp.bfloat16)
    suffix_half = suffix.astype(jnp.bfloat16)
    causal = jnp.arange(tokens_dev)[:, None] >= jnp.arange(tokens_dev)[None, :]
    scores = jnp.where(
        causal,
        jnp.einsum("tghd,sgd->ghts", query_heads, key_heads, preferred_element_type=jnp.float32),
        0.0,
    ).astype(jnp.bfloat16)
    grad_scores = jnp.where(
        causal,
        jnp.einsum("tghe,sge->ghts", grad_heads, value_heads, preferred_element_type=jnp.float32),
        0.0,
    ).astype(jnp.bfloat16)
    grad_query = factor * (
        jnp.einsum("ghts,sgd->tghd", grad_scores, key_heads, preferred_element_type=jnp.float32)
        + jnp.einsum("tghe,gde->tghd", grad_heads, prefix_half, preferred_element_type=jnp.float32)
    )
    grad_key = factor * jnp.einsum(
        "ghts,tghd->sgd", grad_scores, query_heads, preferred_element_type=jnp.float32
    ) + jnp.einsum("sge,gde->sgd", value_heads, suffix_half, preferred_element_type=jnp.float32)
    grad_value = factor * jnp.einsum(
        "ghts,tghe->sge", scores, grad_heads, preferred_element_type=jnp.float32
    ) + jnp.einsum("sgd,gde->sge", key_heads, suffix_half, preferred_element_type=jnp.float32)
    grad_query = grad_query.astype(jnp.bfloat16).reshape(tokens_dev, -1)
    grad_key = grad_key.astype(jnp.bfloat16).reshape(tokens_dev, -1)
    grad_value = grad_value.astype(jnp.bfloat16).reshape(tokens_dev, -1)
    partial_input = (
        contract_rows(grad_query, query_full)
        + contract_rows(grad_key, key_full)
        + contract_rows(grad_value, value_full)
    )
    return lax.psum_scatter(
        partial_input.astype(jnp.bfloat16), "head", scatter_dimension=1, tiled=True
    )


def solution(mesh):
    return jax.shard_map(
        local,
        mesh=mesh,
        in_specs=(
            P("seq", "head"),
            P("seq", "head"),
            P("seq", "head"),
            P("seq", "head"),
            P("seq", "head"),
        ),
        out_specs=P("seq", "head"),
        check_vma=False,
    )
```

profile of v0, /device:TPU:0, one launch (start us, length us, event | category | flops | bytes accessed | tf_op | source)
XLA Modules:
  0.0 408.1 jit_solution(7288737126683894407)
XLA Ops:
  9.4 35.4 %all-gather.9.cloned.1.call-done = bf16[256,4096]{1,0:T(8,128)(2,1)} async-done(((bf16[256,2048]{1,0:T(8,128)(2,1)}), bf16[256,4096]{1,0:T(8,128)(2,1)}) %all-gather.9.cloned.1.call-update) | async-done | bytes 2097168 | tf_op jit(solution)/shard_map/all_gather | solution.py:27
  44.7 52.6 %all-gather.11.cloned.1.call-done = bf16[4096,512]{1,0:T(8,128)(2,1)} async-done(((bf16[256,512]{1,0:T(8,128)(2,1)}), bf16[4096,512]{1,0:T(8,128)(2,1)}) %all-gather.11.cloned.1.call-update) | async-done | bytes 4194320 | tf_op jit(solution)/shard_map/all_gather | solution.py:22
  97.3 4.1 convolution_convert_fusion.2
  101.4 47.0 %all-gather.13.cloned.1.call-done = bf16[4096,512]{1,0:T(8,128)(2,1)} async-done(((bf16[256,512]{1,0:T(8,128)(2,1)}), bf16[4096,512]{1,0:T(8,128)(2,1)}) %all-gather.13.cloned.1.call-update) | async-done | bytes 4194320 | tf_op jit(solution)/shard_map/all_gather | solution.py:23
  148.4 4.1 convolution_convert_fusion.1
  152.5 0.9 convolution_convert_fusion.3
  154.0 121.4 %all-gather.15.cloned.1.call-done = bf16[4096,2048]{1,0:T(8,128)(2,1)} async-done(((bf16[256,2048]{1,0:T(8,128)(2,1)}), bf16[4096,2048]{1,0:T(8,128)(2,1)}) %all-gather.15.cloned.1.call-update) | async-done | bytes 16777232 | tf_op jit(solution)/shard_map/all_gather | solution.py:21
  275.4 10.9 %convolution_convert_fusion = bf16[256,2048]{1,0:T(8,128)(2,1)S(1)} fusion(bf16[256,4096]{1,0:T(8,128)(2,1)} %all-gather.9.cloned.1.call-done, bf16[4096,2048]{1,0:T(8,128)(2,1)} %all-gather.15.cloned.1.call-done), kind=kOutput, calls=%fused_computation.7 | convolution fusion | flops 4295491584 | bytes 19922944 | tf_op jit(solution)/shard_map/dot_general | solution.py:29
  286.9 1.1 fusion.18
  289.0 0.8 reshape.39
  289.8 0.8 reshape.21
  290.5 2.0 fusion.2
  292.6 1.8 fusion.24
  294.4 22.7 %all-gather.17.cloned.1.call-done = bf16[64,128,128]{2,1,0:T(8,128)(2,1)} async-done(((bf16[4,128,128]{2,1,0:T(8,128)(2,1)}), bf16[64,128,128]{2,1,0:T(8,128)(2,1)}) %all-gather.17.cloned.1.call-update) | async-done | bytes 2097168 | tf_op jit(solution)/shard_map/all_gather | solution.py:45
  317.1 3.0 fusion.7
  320.0 3.0 fusion.4
  323.1 3.4 fusion.14
  326.5 1.6 fusion.12
  328.1 12.8 %fusion.43 = f32[256,4096]{1,0:T(8,128)} fusion(bf16[256,2048]{0,1:T(8,128)(2,1)} %bitcast.137, bf16[4096,2048]{1,0:T(8,128)(2,1)} %all-gather.15.cloned.1.call-done), kind=kOutput, calls=%fused_computation.57 | convolution fusion | flops 4294967296 | bytes 22020096 | tf_op jit(solution)/shard_map/dot_general | solution.py:12
  340.9 18.4 %all-gather.19.cloned.1.call-done = bf16[64,128,128]{2,1,0:T(8,128)(2,1)} async-done(((bf16[4,128,128]{2,1,0:T(8,128)(2,1)}), bf16[64,128,128]{2,1,0:T(8,128)(2,1)}) %all-gather.19.cloned.1.call-update) | async-done | bytes 2097168 | tf_op jit(solution)/shard_map/all_gather | solution.py:46
  359.3 2.9 fusion.5
  362.9 4.9 %convolution_add_fusion.1 = f32[256,4096]{1,0:T(8,128)S(1)} fusion(f32[256,4096]{1,0:T(8,128)} %fusion.43, bf16[256,512]{0,1:T(8,128)(2,1)S(1)} %bitcast.140, bf16[4096,512]{1,0:T(8,128)(2,1)} %all-gather.11.cloned.1.call-done), kind=kOutput, calls=%fused_computation.1 | convolution fusion | flops 1074790400 | bytes 12845056 | tf_op jit(solution)/shard_map/dot_general | solution.py:12
  367.8 2.7 fusion
  370.5 30.8 %reduce-scatter.2.cloned.1.call-done = bf16[256,2048]{1,0:T(8,128)(2,1)} async-done(((bf16[256,4096]{1,0:T(8,128)(2,1)}), bf16[256,2048]{1,0:T(8,128)(2,1)}) %reduce-scatter.2.cloned.1.call-update) | async-done | bytes 1048592 | tf_op jit(solution)/shard_map/reduce_scatter | solution.py:85
  (41 shorter events, 5.6 us)
Async XLA Ops:
  6.5 38.2 %all-gather.9.cloned.1.call-start = ((), (), s32[]{:S(2)}) async-start(), calls=%async_computation.1 | async-start | bytes 3145728 | tf_op jit(solution)/shard_map/all_gather | solution.py:27
  7.3 90.0 %all-gather.11.cloned.1.call-start = ((), (), s32[]{:S(2)}) async-start(), calls=%async_computation.2 | async-start | bytes 4456448 | tf_op jit(solution)/shard_map/all_gather | solution.py:22
  8.0 140.4 %all-gather.13.cloned.1.call-start = ((), (), s32[]{:S(2)}) async-start(), calls=%async_computation.3 | async-start | bytes 4456448 | tf_op jit(solution)/shard_map/all_gather | solution.py:23
  8.7 266.7 %all-gather.15.cloned.1.call-start = ((), (), s32[]{:S(2)}) async-start(), calls=%async_computation.4 | async-start | bytes 17825792 | tf_op jit(solution)/shard_map/all_gather | solution.py:21
  9.3 307.8 %all-gather.17.cloned.1.call-start = ((), (), s32[]{:S(2)}) async-start(), calls=%async_computation.6 | async-start | bytes 2228224 | tf_op jit(solution)/shard_map/all_gather | solution.py:45
  101.4 52.1 %copy-start.5 = (bf16[256,2048]{1,0:T(8,128)(2,1)S(1)}, bf16[256,2048]{1,0:T(8,128)(2,1)}, u32[]{:S(2)}) copy-start(bf16[256,2048]{1,0:T(8,128)(2,1)} %param.6) | copy-start | bytes 3145732
  152.5 1.0 copy-start.6
  153.4 205.9 %all-gather.19.cloned.1.call-start = ((), (), s32[]{:S(2)}) async-start(), calls=%async_computation.7 | async-start | bytes 2228224 | tf_op jit(solution)/shard_map/all_gather | solution.py:46
  154.0 132.8 %copy-start = (bf16[256,2048]{0,1:T(8,128)(2,1)}, bf16[256,2048]{0,1:T(8,128)(2,1)S(1)}, u32[]{:S(2)}) copy-start(bf16[256,2048]{0,1:T(8,128)(2,1)S(1)} %copy.60) | copy-start | bytes 3145732
  286.8 1.4 copy-start.7
  288.0 113.3 %reduce-scatter.2.cloned.1.call-start = ((), (), s32[]{:S(2)}) async-start(), calls=%async_computation.5 | async-start | bytes 3145728 | tf_op jit(solution)/shard_map/reduce_scatter | solution.py:85
  290.5 2.0 copy-start.4
  317.1 3.0 copy-start.1
  340.9 21.5 %copy-start.9 = (f32[256,4,128]{0,2,1:T(8,128)S(1)}, f32[256,4,128]{0,2,1:T(8,128)}, u32[]{:S(2)}) copy-start(f32[256,4,128]{0,2,1:T(8,128)} %fusion.14) | copy-start | bytes 1572868
  340.9 21.7 %copy-start.3 = (f32[4,128,256]{2,1,0:T(8,128)S(1)}, f32[4,128,256]{2,1,0:T(8,128)}, u32[]{:S(2)}) copy-start(f32[4,128,256]{2,1,0:T(8,128)} %fusion.12) | copy-start | bytes 1572868
  340.9 21.7 %copy-start.8 = (bf16[256,512]{1,0:T(8,128)(2,1)S(1)}, bf16[256,512]{1,0:T(8,128)(2,1)}, u32[]{:S(2)}) copy-start(bf16[256,512]{1,0:T(8,128)(2,1)} %copy-done.6) | copy-start | bytes 786436
  362.9 4.9 %copy-start.2 = (bf16[4096,512]{1,0:T(8,128)(2,1)S(1)}, bf16[4096,512]{1,0:T(8,128)(2,1)}, u32[]{:S(2)}) copy-start(bf16[4096,512]{1,0:T(8,128)(2,1)} %all-gather.13.cloned.1.call-done) | copy-start | bytes 12582916
Sparse Core Ops, SparseCore 0:
  8.9 35.8 all-gather.8
  46.9 50.3 all-gather.10
  99.5 48.8 all-gather.12
  150.4 124.9 all-gather.14
  277.4 39.6 all-gather.16
  319.1 40.1 all-gather.18
  370.6 30.6 reduce-scatter.1
where the time goes:
time: 408 us
  waiting for transfers between devices  331 us (81%)
  matrix products  59.6 us (15%)
  between operations  13.7 us (3%)
    all_gather x1, waiting for transfers between devices, local(): lax.all_gather(query_weight, 'seq', axis=0, tiled=True)  121 us
    all_gather x1, waiting for transfers between devices, local(): lax.all_gather(key_weight, 'seq', axis=0, tiled=True)  52.6 us
    all_gather x1, waiting for transfers between devices, local(): lax.all_gather(value_weight, 'seq', axis=0, tiled=True)  47 us
    all_gather x1, waiting for transfers between devices, local(): portion = lax.all_gather(activations, 'head', axis=1, tiled=True)  35.4 us
    reduce_scatter x1, waiting for transfers between devices, local(): lax.psum_scatter(partial_input.astype(jnp.bfloat16), 'head', scatter_dime...  30.8 us
    all_gather x1, waiting for transfers between devices, local(): lax.all_gather(kv_state[None], 'seq', axis=0, tiled=True)  22.7 us
    dot_general x3, matrix products, contract_rows(): lax.dot_general(grads, weight, (((1,), (1,)), ((), ())), preferred_elemen...  20.4 us
    dot_general x3, matrix products, local(): jnp.dot(portion, weight, preferred_element_type=jnp.float32)  19 us
  transfers between devices with their start and end apart: 7, of which 7 were waited for; matrix products, arithmetic and copies ran while one was open for 13% of the time, Pallas kernels for 0%

commit v1 on v0

v1 whole, which is shorter than its diff:
```python
import jax
import jax.numpy as jnp
from jax import lax
from jax.experimental import pallas as pl
from jax.experimental.pallas import tpu as pltpu
from jax.sharding import PartitionSpec as P


HEADS = 32
KV_HEADS = 8
HEAD_DIM = 128
GROUP = HEADS // KV_HEADS
FACTOR = HEAD_DIM ** (-0.5)
F32 = jnp.float32
BF16 = jnp.bfloat16


def dot_nt(a, b):
    return lax.dot_general(a, b, (((1,), (1,)), ((), ())), preferred_element_type=F32)


def make_plain():
    def local(activations, grad_out, query_weight, key_weight, value_weight):
        gathered = tuple(
            lax.all_gather(w, "seq", axis=0, tiled=True)
            for w in (query_weight, key_weight, value_weight)
        )
        tokens = activations.shape[0]
        whole = lax.all_gather(activations, "head", axis=1, tiled=True)
        queries, keys, values = (
            jnp.dot(whole, w, preferred_element_type=F32).astype(BF16) for w in gathered
        )
        groups = keys.shape[1] // HEAD_DIM
        q = queries.reshape(tokens, groups, GROUP, HEAD_DIM)
        k = keys.reshape(tokens, groups, HEAD_DIM)
        v = values.reshape(tokens, groups, HEAD_DIM)
        do = grad_out.reshape(tokens, groups, GROUP, HEAD_DIM)
        kv_state = jnp.einsum("tgd,tge->gde", k, v, preferred_element_type=F32).astype(BF16)
        grad_state = (
            FACTOR * jnp.einsum("tghd,tghe->gde", q, do, preferred_element_type=F32)
        ).astype(BF16)
        every_kv = lax.all_gather(kv_state[None], "seq", axis=0, tiled=True)
        every_grad = lax.all_gather(grad_state[None], "seq", axis=0, tiled=True)
        position = lax.axis_index("seq")
        order = jnp.arange(every_kv.shape[0], dtype=jnp.int32)
        before = (order < position).astype(BF16)
        after = (order > position).astype(BF16)
        prefix = jnp.einsum("n,ngde->gde", before, every_kv, preferred_element_type=F32).astype(BF16)
        suffix = jnp.einsum("n,ngde->gde", after, every_grad, preferred_element_type=F32).astype(BF16)
        causal = jnp.arange(tokens)[:, None] >= jnp.arange(tokens)[None, :]
        s = jnp.where(
            causal, jnp.einsum("tghd,sgd->ghts", q, k, preferred_element_type=F32), 0.0
        ).astype(BF16)
        ds = jnp.where(
            causal, jnp.einsum("tghe,sge->ghts", do, v, preferred_element_type=F32), 0.0
        ).astype(BF16)
        grad_query = FACTOR * (
            jnp.einsum("ghts,sgd->tghd", ds, k, preferred_element_type=F32)
            + jnp.einsum("tghe,gde->tghd", do, prefix, preferred_element_type=F32)
        )
        grad_key = FACTOR * jnp.einsum(
            "ghts,tghd->sgd", ds, q, preferred_element_type=F32
        ) + jnp.einsum("sge,gde->sgd", v, suffix, preferred_element_type=F32)
        grad_value = FACTOR * jnp.einsum(
            "ghts,tghe->sge", s, do, preferred_element_type=F32
        ) + jnp.einsum("sgd,gde->sge", k, suffix, preferred_element_type=F32)
        parts = (
            dot_nt(g.astype(BF16).reshape(tokens, -1), w)
            for g, w in zip((grad_query, grad_key, grad_value), gathered)
        )
        return lax.psum_scatter(
            sum(parts).astype(BF16), "head", scatter_dimension=1, tiled=True
        )

    return local


def mm(a, b, contract):
    return lax.dot_general(a, b, (contract, ((), ())), preferred_element_type=F32)


NN, NT, TN = ((1,), (0,)), ((1,), (1,)), ((0,), (0,))


def causal_mask(n):
    return lax.broadcasted_iota(jnp.int32, (n, n), 0) >= lax.broadcasted_iota(
        jnp.int32, (n, n), 1
    )


def head_cols(h):
    return slice(h * HEAD_DIM, (h + 1) * HEAD_DIM)


def state_kernel(kv_ref, out_ref, total_ref):
    tokens = kv_ref.shape[0] // 2
    for g in range(out_ref.shape[1]):
        total = jnp.zeros(total_ref.shape[1:], F32)
        for n in range(out_ref.shape[0]):
            t = slice(n * tokens, (n + 1) * tokens)
            k, v = kv_ref[t, head_cols(2 * g)], kv_ref[t, head_cols(2 * g + 1)]
            state = mm(k, v, TN).astype(BF16)
            out_ref[n, g] = state
            total = total + state.astype(F32)
        total_ref[g] = total.astype(BF16)


def grad_query_kernel(k_ref, v_ref, do_ref, prefix_ref, out_ref):
    k, v, prefix = k_ref[...], v_ref[...], prefix_ref[0, 0]
    mask = causal_mask(k.shape[0])
    for h in range(GROUP):
        do = do_ref[:, head_cols(h)]
        ds = jnp.where(mask, mm(do, v, NT), 0.0).astype(BF16)
        out_ref[:, head_cols(h)] = (FACTOR * (mm(ds, k, NN) + mm(do, prefix, NT))).astype(BF16)


def inner_kernel(q_ref, k_ref, v_ref, do_ref, out_ref):
    k, v = k_ref[...], v_ref[...]
    shape = (k.shape[0], k.shape[0])
    mask = lax.broadcasted_iota(jnp.int32, shape, 0) <= lax.broadcasted_iota(jnp.int32, shape, 1)
    gk = jnp.zeros(k.shape, F32)
    gv = jnp.zeros(k.shape, F32)
    for h in range(GROUP):
        q, do = q_ref[:, head_cols(h)], do_ref[:, head_cols(h)]
        ds = jnp.where(mask, mm(v, do, NT), 0.0).astype(BF16)
        s = jnp.where(mask, mm(k, q, NT), 0.0).astype(BF16)
        gk = gk + mm(ds, q, NN)
        gv = gv + mm(s, do, NN)
    out_ref[:, head_cols(0)] = FACTOR * gk
    out_ref[:, head_cols(1)] = FACTOR * gv


def outer_kernel(flag_ref, kv_ref, outside_ref, got_ref, state_ref, *refs):
    inner_refs, out_refs = refs[:-2], refs[-2:]
    tokens = kv_ref.shape[0] // 2
    for g, inner_ref in enumerate(inner_refs):
        behind = outside_ref[g] + jnp.where(flag_ref[0] == 1, got_ref[g].astype(F32), 0.0)
        for n in range(2):
            add = (flag_ref[1] == 1) if n == 0 else (flag_ref[1] == 0)
            suffix = behind + jnp.where(add, state_ref[1 - n, g].astype(F32), 0.0)
            suffix = suffix.astype(BF16)
            t = slice(n * tokens, (n + 1) * tokens)
            k, v = kv_ref[t, head_cols(2 * g)], kv_ref[t, head_cols(2 * g + 1)]
            gk = inner_ref[t, head_cols(0)] + mm(v, suffix, NT)
            gv = inner_ref[t, head_cols(1)] + mm(k, suffix, NN)
            out_refs[n][:, head_cols(2 * g)] = gk.astype(BF16)
            out_refs[n][:, head_cols(2 * g + 1)] = gv.astype(BF16)


def project_call(base, x, weights, total, dtype, do=None):
    slots = sorted(weights)
    rows, cols = weights[slots[0]].shape
    tokens = x.shape[0] // 2
    width = GROUP * HEAD_DIM if do is not None else rows // 2
    n = len(slots)

    def body(base_ref, *refs):
        xs, ws = refs[:n], refs[n : 2 * n]
        rest = list(refs[2 * n :])
        acc = rest.pop(0)[...] if total is not None else None
        do_ref = rest.pop(0) if do is not None else None
        for x_ref, w_ref in zip(xs, ws):
            part = mm(x_ref[...], w_ref[...], NN)
            acc = part if acc is None else acc + part
        acc = acc.astype(dtype)
        rest[0][...] = acc
        if do_ref is not None:
            both = None
            for m in range(2):
                t = slice(m * tokens, (m + 1) * tokens)
                state = None
                for h in range(GROUP):
                    part = mm(acc[t, head_cols(h)], do_ref[t, head_cols(h)], TN)
                    state = part if state is None else state + part
                state = (FACTOR * state).astype(BF16)
                rest[1][m, 0] = state
                state = state.astype(F32)
                both = state if both is None else both + state
            rest[2][0] = both.astype(BF16)

    def x_spec(i):
        return pl.BlockSpec((2 * tokens, rows), lambda j, b: (0, b[0] ^ i))

    tile = pl.BlockSpec((2 * tokens, width), lambda j, b: (0, j))
    args = [x] * n + [weights[i] for i in slots]
    in_specs = [x_spec(i) for i in slots]
    in_specs += [pl.BlockSpec((rows, width), lambda j, b: (0, j))] * n
    out_shape, out_specs = [jax.ShapeDtypeStruct((2 * tokens, cols), dtype)], [tile]
    if total is not None:
        args.append(total)
        in_specs.append(tile)
    if do is not None:
        args.append(do)
        in_specs.append(tile)
        one = (cols // width, HEAD_DIM, HEAD_DIM)
        out_shape += [jax.ShapeDtypeStruct((2,) + one, BF16), jax.ShapeDtypeStruct(one, BF16)]
        out_specs += [
            pl.BlockSpec((2, 1, HEAD_DIM, HEAD_DIM), lambda j, b: (0, j, 0, 0)),
            pl.BlockSpec((1, HEAD_DIM, HEAD_DIM), lambda j, b: (j, 0, 0)),
        ]
    out = pl.pallas_call(
        body,
        out_shape=out_shape,
        grid_spec=pltpu.PrefetchScalarGridSpec(
            num_scalar_prefetch=1,
            grid=(cols // width,),
            in_specs=in_specs,
            out_specs=out_specs,
        ),
    )(base, *args)
    return out if do is not None else out[0]


def back_call(side, grads, low, high):
    weights = low + high
    n = len(low)
    rows, inner = weights[0].shape
    tokens = grads.shape[0] // 2
    half = rows // 2

    def body(side_ref, g_ref, *refs):
        ws, (keep_ref, send_ref) = refs[:-2], refs[-2:]
        for m, w_ref in enumerate(ws):

            @pl.when(pl.program_id(0) == m)
            def _():
                both = mm(g_ref[...], w_ref[...], NT)
                keep_ref[0] = both[:tokens]
                send_ref[0] = both[tokens:].astype(BF16)

    def w_spec(m):
        return pl.BlockSpec(
            (half, inner),
            lambda i, j, b: (jnp.where(i == m, j, jnp.where(i < m, 0, 1)), 0),
        )

    out = pl.BlockSpec(
        (1, tokens, half), lambda i, j, b: ((i // n) ^ b[0], 0, (i % n) * 2 + j)
    )
    shape = (2, tokens, n * rows)
    return pl.pallas_call(
        body,
        out_shape=(jax.ShapeDtypeStruct(shape, F32), jax.ShapeDtypeStruct(shape, BF16)),
        grid_spec=pltpu.PrefetchScalarGridSpec(
            num_scalar_prefetch=1,
            grid=(2 * n, 2),
            in_specs=[pl.BlockSpec(grads.shape, lambda i, j, b: (0, 0))]
            + [w_spec(m) for m in range(2 * n)],
            out_specs=(out, out),
        ),
    )(side, grads, *weights)


def finish_kernel(base_ref, sum_ref, g_ref, w_ref, w_other_ref, out_ref):
    n = w_ref.shape[1]
    total = sum_ref[...] + mm(g_ref[:, :n], w_ref[...], NT)
    out_ref[...] = (total + mm(g_ref[:, n:], w_other_ref[...], NT)).astype(BF16)


def make_split(zs, xs, ys):
    n_seq = zs * xs * 2

    def swap(value, bit):
        return lax.ppermute(value, "seq", [(s, s ^ bit) for s in range(n_seq)])

    def swap_y(value):
        return lax.ppermute(value, "head", [(y, y ^ 1) for y in range(ys)])

    Z1, Z2, X1, C1 = 2 * xs, 4 * xs, 2, 1

    def local(activations, grad_out, query_weight, key_weight, value_weight):
        tokens, _ = activations.shape
        groups = key_weight.shape[1] // HEAD_DIM // 2
        seq = lax.axis_index("seq")
        y = lax.axis_index("head")
        core, x, z = seq % 2, (seq // 2) % xs, seq // (2 * xs)
        chip, chips = seq // 2, n_seq // 2
        per_half = chips // ys
        side = (chip // per_half) ^ y

        def cols(w, which):
            n = w.shape[1] // 2
            return lax.dynamic_slice_in_dim(w, which * n, n, 1)

        def own_and_other(own, other):
            return jnp.concatenate([own, swap(other, C1)], 0)

        def in_order(own, other):
            n = own.shape[0]
            both = jnp.zeros((2 * n, own.shape[1]), own.dtype)
            both = lax.dynamic_update_slice_in_dim(both, own, core * n, 0)
            got = swap(other, C1)
            return lax.dynamic_update_slice_in_dim(both, got, (1 - core) * n, 0)

        def keys_and_values(which):
            k, v = cols(key_weight, which), cols(value_weight, which)
            return jnp.concatenate(
                [w[:, head_cols(g)] for g in range(groups) for w in (k, v)], 1
            )

        def scalar(value):
            return value.reshape(1).astype(jnp.int32)

        chunk_a = in_order(keys_and_values(core), keys_and_values(1 - core))
        chunk_b = in_order(cols(query_weight, core), cols(query_weight, 1 - core))
        do_all = own_and_other(cols(grad_out, core), cols(grad_out, 1 - core))
        acts = jnp.concatenate([activations, swap_y(activations)], 1)
        acts = own_and_other(acts, acts)
        base = scalar(side * per_half + chip % per_half)

        def project(weights, which, total, dtype, do=None):
            return project_call(
                base, acts, {i: weights[i] for i in which}, total, dtype, do
            )

        w_kv, w_q = [chunk_a] + [None] * (chips - 1), [chunk_b] + [None] * (chips - 1)
        w_kv[4], w_kv[2] = swap(chunk_a, Z2), swap(chunk_a, Z1)
        w_kv[1], w_q[1] = swap(chunk_a, X1), swap(chunk_b, X1)
        w_kv[6] = swap(w_kv[4], Z1)
        w_q[4], w_q[2] = swap(chunk_b, Z2), swap(chunk_b, Z1)
        w_kv[3], w_kv[5] = swap(w_kv[2], X1), swap(w_kv[4], X1)
        w_kv[7] = swap(w_kv[6], X1)
        kv_sum = project(w_kv, (0, 1, 2, 4), None, F32)
        w_q[5], w_q[6] = swap(w_q[4], X1), swap(w_q[4], Z1)
        kv = project(w_kv, (3, 5, 6, 7), kv_sum, BF16)
        w_q[3] = swap(w_q[2], X1)
        q_sum = project(w_q, (0, 1, 2, 4), None, F32)
        cut = chunk_b.shape[0] * 3 // 8
        w_q[7] = jnp.concatenate([swap(w_q[6][:cut], X1), swap(w_q[5][cut:], Z1)], 0)

        n_half = chips // ys
        low, high = jnp.concatenate(w_kv[:n_half], 0), jnp.concatenate(w_kv[n_half:], 0)
        w_home = jnp.where(side == 0, low, high)
        w_home_y = swap_y(jnp.where(side == 0, high, low))
        w_home_c = swap(w_home, C1)
        w_home_cy = swap(w_home_y, C1)

        n_cols = GROUP * HEAD_DIM
        states = jax.ShapeDtypeStruct((2, groups, HEAD_DIM, HEAD_DIM), BF16)

        def scan(total, ahead):
            total = total.astype(F32)
            outside = jnp.zeros_like(total)
            for bit, at in ((X1, x), (Z1, z % 2), (Z2, z // 2)):
                got = swap(total.astype(BF16), bit)
                counts = (at == 1) == ahead
                if bit == Z2:
                    return outside, got, counts
                outside = outside + jnp.where(counts, got.astype(F32), 0.0)
                total = total + got.astype(F32)

        totals = jax.ShapeDtypeStruct(states.shape[1:], BF16)
        state, total = pl.pallas_call(state_kernel, out_shape=(states, totals))(kv)
        outside, got, counts = scan(total, True)
        outside = outside + jnp.where(counts, got.astype(F32), 0.0)
        prefix = jnp.stack(
            [
                outside + jnp.where(core == 1, state[1].astype(F32), 0.0),
                outside + jnp.where(core == 0, state[0].astype(F32), 0.0),
            ]
        ).astype(BF16)
        q_spec = pl.BlockSpec((tokens, n_cols), lambda n, g: (n, g))
        gq = pl.pallas_call(
            grad_query_kernel,
            out_shape=jax.ShapeDtypeStruct((2 * tokens, groups * n_cols), BF16),
            grid=(2, groups),
            in_specs=[
                pl.BlockSpec((tokens, HEAD_DIM), lambda n, g: (n, 2 * g)),
                pl.BlockSpec((tokens, HEAD_DIM), lambda n, g: (n, 2 * g + 1)),
                q_spec,
                pl.BlockSpec((1, 1, HEAD_DIM, HEAD_DIM), lambda n, g: (n, g, 0, 0)),
            ],
            out_specs=q_spec,
        )(kv, kv, do_all, prefix)

        def back(which):
            keep, send = back_call(
                scalar(side), gq, [w_q[i] for i in which], [w_q[i + n_half] for i in which]
            )
            got = swap(send, C1)
            away = (keep[1] + got[1].astype(F32)).astype(BF16)
            return keep[0], got[0], swap_y(away)

        early = back(range(n_half - 1))
        q_sum = project(w_q, (5, 6), q_sum, F32)
        q, gs, total = project(w_q, (3, 7), q_sum, BF16, do_all)
        outside, got, counts = scan(total, False)
        inner = []
        for g in range(groups):
            inner.append(
                pl.pallas_call(
                    inner_kernel,
                    out_shape=jax.ShapeDtypeStruct((2 * tokens, 2 * HEAD_DIM), F32),
                    grid=(2,),
                    in_specs=[
                        pl.BlockSpec((tokens, n_cols), lambda n, g=g: (n, g)),
                        pl.BlockSpec((tokens, HEAD_DIM), lambda n, g=g: (n, 2 * g)),
                        pl.BlockSpec((tokens, HEAD_DIM), lambda n, g=g: (n, 2 * g + 1)),
                        pl.BlockSpec((tokens, n_cols), lambda n, g=g: (n, g)),
                    ],
                    out_specs=pl.BlockSpec((tokens, 2 * HEAD_DIM), lambda n: (n, 0)),
                )(q, kv, kv, do_all)
            )
        late = back((n_half - 1,))
        flags = jnp.stack([counts, core == 0]).astype(jnp.int32)
        part = jax.ShapeDtypeStruct((tokens, 2 * groups * HEAD_DIM), BF16)
        vmem = pl.BlockSpec(memory_space=pltpu.VMEM)
        gkv, gkv_other = pl.pallas_call(
            outer_kernel,
            out_shape=(part, part),
            in_specs=[pl.BlockSpec(memory_space=pltpu.SMEM)] + [vmem] * (4 + groups),
            out_specs=(vmem, vmem),
        )(flags, kv, outside, got, gs, *inner)
        gkv_c = swap(gkv_other, C1)
        far = swap_y(jnp.concatenate([gkv, gkv_c], 1))
        home = jnp.concatenate(
            [p[0] + p[1].astype(F32) + p[2].astype(F32) for p in (early, late)], 1
        )
        home = home + mm(gkv, w_home, NT) + mm(gkv_c, w_home_c, NT)
        width = home.shape[1] // n_half
        w_spec = pl.BlockSpec((width, w_home.shape[1]), lambda i, b: (b[0] ^ i, 0))
        return pl.pallas_call(
            finish_kernel,
            out_shape=jax.ShapeDtypeStruct(home.shape, BF16),
            grid_spec=pltpu.PrefetchScalarGridSpec(
                num_scalar_prefetch=1,
                grid=(n_half,),
                in_specs=[
                    pl.BlockSpec((tokens, width), lambda i, b: (0, b[0] ^ i)),
                    pl.BlockSpec(far.shape, lambda i, b: (0, 0)),
                    w_spec,
                    w_spec,
                ],
                out_specs=pl.BlockSpec((tokens, width), lambda i, b: (0, i)),
            ),
        )(scalar(chip % per_half), home, far, w_home_y, w_home_cy)

    return local


def solution(mesh):
    n_seq, n_head = mesh.shape["seq"], mesh.shape["head"]
    groups = KV_HEADS // n_head
    split = n_seq == 4 * 2 * 2 and groups % 2 == 0 and n_head == 2
    local = make_split(n_seq // 4, 2, n_head) if split else make_plain()

    spec = P("seq", "head")
    return jax.shard_map(local, mesh=mesh, in_specs=(spec,) * 5, out_specs=spec, check_vma=False)
```

time: 408 us -> 315 us (0.77)
  waiting for transfers between devices: 331 us -> 177 us
  Pallas kernels: 0 us -> 65.6 us
  matrix products: 59.6 us -> 4.64 us
  starting transfers between devices: 0.42 us -> 29.3 us
  other arithmetic: 0.03 us -> 18.6 us
  local copies, waits for them, and re-layouts: 3.51 us -> 18.4 us
  between operations: 13.7 us -> 0.35 us
    all_gather x6 -> x0, waiting for transfers between devices: 297 us -> none  [the longest x1 121 us: local(): lax.all_gather(query_weight, 'seq', axis=0, tiled=True)]
    ppermute x0 -> x35, waiting for transfers between devices: none -> 177 us  [the longest x30 126 us: swap(): return lax.ppermute(value, 'seq', [(s, s ^ bit) for s in range(n_seq)])]
    pallas_call x0 -> x13, Pallas kernels: none -> 65.6 us  [the longest x5 25.5 us: project_call(): pl.pallas_call(body, out_shape=out_shape, grid_spec=pltpu.PrefetchScalarG...]
    dot_general x17 -> x2, matrix products: 59.6 us -> 4.64 us  [mm(): lax.dot_general(a, b, (contract, ((), ())), preferred_element_type=F32)]
    reduce_scatter x1 -> x0, waiting for transfers between devices: 30.8 us -> none  [local(): lax.psum_scatter(partial_input.astype(jnp.bfloat16), 'head', scatter_dime...]
    ppermute x0 -> x35, starting transfers between devices: none -> 29.3 us  [the longest x30 22.1 us: swap(): return lax.ppermute(value, 'seq', [(s, s ^ bit) for s in range(n_seq)])]
    unnamed x20 -> x45, local copies, waits for them, and re-layouts: 0.04 us -> 7.03 us
    concatenate x0 -> x4, other arithmetic: none -> 6.9 us  [the longest x2 6.82 us: own_and_other(): return jnp.concatenate([own, swap(other, C1)], 0)]
  transfers between devices with their start and end apart: 7 -> 35, of which waited for: 7 -> 14; matrix products, arithmetic and copies ran while one was open for 13% -> 12% of each run, Pallas kernels for 0% -> 19%
where the time goes in v1:
time: 315 us; the launch traced here: 314 us
  waiting for transfers between devices  177 us (56%)
  Pallas kernels  65.6 us (21%)
  starting transfers between devices  29.3 us (9%)
  other arithmetic  18.6 us (6%)
  local copies, waits for them, and re-layouts  18.4 us (6%)
  matrix products  4.64 us (1%)
    ppermute x30, waiting for transfers between devices, swap(): return lax.ppermute(value, 'seq', [(s, s ^ bit) for s in range(n_seq)])  126 us
    ppermute x5, waiting for transfers between devices, swap_y(): return lax.ppermute(value, 'head', [(y, y ^ 1) for y in range(ys)])  50.6 us
    pallas_call x5, Pallas kernels, project_call(): pl.pallas_call(body, out_shape=out_shape, grid_spec=pltpu.PrefetchScalarG...  25.5 us
    ppermute x30, starting transfers between devices, swap(): return lax.ppermute(value, 'seq', [(s, s ^ bit) for s in range(n_seq)])  22.1 us
    pallas_call x2, Pallas kernels, back_call(): pl.pallas_call(body, out_shape=(jax.ShapeDtypeStruct(shape, F32), jax.Sha...  17.9 us
    ppermute x5, starting transfers between devices, swap_y(): return lax.ppermute(value, 'head', [(y, y ^ 1) for y in range(ys)])  7.24 us
    pallas_call x2, Pallas kernels, local(): pl.pallas_call(inner_kernel, out_shape=jax.ShapeDtypeStruct((2 * tokens,...  7.15 us
    unnamed x45, local copies, waits for them, and re-layouts  7.03 us
  transfers between devices with their start and end apart: 35, of which 14 were waited for; matrix products, arithmetic and copies ran while one was open for 12% of the time, Pallas kernels for 19%

profile of v1, /device:TPU:0, one launch (start us, length us, event | category | flops | bytes accessed | tf_op | source)
XLA Modules:
  0.0 313.9 jit_solution(348515589038712595)
XLA Ops:
  5.4 21.0 %collective-permute-done = bf16[256,2048]{1,0:T(8,128)(2,1)S(1)} collective-permute-done((bf16[256,2048]{1,0:T(8,128)(2,1)}, bf16[256,2048]{1,0:T(8,128)(2,1)S(1)}, u32[]{:S(2)}, u32[]{:S(2)}) %collective-permute-start) | collective-permute-done | bytes 1048608 | tf_op jit(solution)/shard_map/ppermute | solution.py:267
  28.2 3.9 %collective-permute-done.2 = bf16[256,512]{1,0:T(8,128)(2,1)S(1)} collective-permute-done((bf16[256,512]{1,0:T(8,128)(2,1)S(1)}, bf16[256,512]{1,0:T(8,128)(2,1)S(1)}, u32[]{:S(2)}, u32[]{:S(2)}) %collective-permute-start.2) | collective-permute-done | bytes 262176 | tf_op jit(solution)/shard_map/ppermute | solution.py:264
  36.1 22.4 %collective-permute-done.5.refs_7_ = bf16[512,512]{1,0:T(8,128)(2,1)S(1)} collective-permute-done((bf16[512,512]{1,0:T(8,128)(2,1)S(1)}, bf16[512,512]{1,0:T(8,128)(2,1)S(1)}, u32[]{:S(2)}, u32[]{:S(2)}) %collective-permute-start.5) | collective-permute-done | bytes 524320 | tf_op jit(solution)/shard_map/ppermute | solution.py:264
  63.7 9.7 %collective-permute-done.6.refs_5_ = bf16[512,512]{1,0:T(8,128)(2,1)} collective-permute-done((bf16[512,512]{1,0:T(8,128)(2,1)S(1)}, bf16[512,512]{1,0:T(8,128)(2,1)}, u32[]{:S(2)}, u32[]{:S(2)}) %collective-permute-start.6) | collective-permute-done | bytes 524320 | tf_op jit(solution)/shard_map/ppermute | solution.py:264
  76.8 10.6 %collective-permute-done.7.refs_6_ = bf16[512,512]{1,0:T(8,128)(2,1)} collective-permute-done((bf16[512,512]{1,0:T(8,128)(2,1)S(1)}, bf16[512,512]{1,0:T(8,128)(2,1)}, u32[]{:S(2)}, u32[]{:S(2)}) %collective-permute-start.7) | collective-permute-done | bytes 524320 | tf_op jit(solution)/shard_map/ppermute | solution.py:264
  88.6 8.3 %collective-permute-done.3.refs_6_ = bf16[512,512]{1,0:T(8,128)(2,1)S(1)} collective-permute-done((bf16[512,512]{1,0:T(8,128)(2,1)S(1)}, bf16[512,512]{1,0:T(8,128)(2,1)S(1)}, u32[]{:S(2)}, u32[]{:S(2)}) %collective-permute-start.3) | collective-permute-done | bytes 524320 | tf_op jit(solution)/shard_map/ppermute | solution.py:264
  99.0 4.7 %pad_maximum_fusion.refs_0_.refs_1_.refs_2_.refs_3_ = bf16[512,4096]{1,0:T(8,128)(2,1)} fusion(bf16[256,4096]{1,0:T(8,128)(2,1)} %collective-permute-done.1, bf16[256,4096]{1,0:T(8,128)(2,1)} %constant_dynamic-update-slice_fusion), kind=kLoop, calls=%fused_computation | loop fusion | flops 8388608 | bytes 8388608 | tf_op jit(solution)/shard_map/concatenate | solution.py:286
  103.7 4.4 %shard_map.55.refs_8_ = f32[512,512]{1,0:T(8,128)} custom-call(s32[1]{0:T(128)} %bitcast.2.base_ref, bf16[512,4096]{1,0:T(8,128)(2,1)} %pad_maximum_fusion.refs_0_.refs_1_.refs_2_.refs_3_, bf16[512,4096]{1,0:T(8,128)(2,1)} %pad_maximum_fusion.refs_0_.refs_1_.refs_2_.refs_3_, bf16[512,4096]{1,0:T(8,128)(2,1)} %pad_maximum_fusion.refs_0_.refs_1_.refs_2_.refs_3_, ...), custom_call_target="tpu_custom_call" | custom-call | tf_op jit(solution)/shard_map/pallas_call | solution.py:201
  108.1 3.6 %collective-permute-done.4.refs_4_ = bf16[512,512]{1,0:T(8,128)(2,1)S(1)} collective-permute-done((bf16[512,512]{1,0:T(8,128)(2,1)S(1)}, bf16[512,512]{1,0:T(8,128)(2,1)S(1)}, u32[]{:S(2)}, u32[]{:S(2)}) %collective-permute-start.4) | collective-permute-done | bytes 524320 | tf_op jit(solution)/shard_map/ppermute | solution.py:264
  111.7 7.5 %collective-permute-done.17.refs_3_.refs_7_ = bf16[512,1024]{1,0:T(8,128)(2,1)} collective-permute-done((bf16[512,1024]{1,0:T(8,128)(2,1)S(1)}, bf16[512,1024]{1,0:T(8,128)(2,1)}, u32[]{:S(2)}, u32[]{:S(2)}) %collective-permute-start.17) | collective-permute-done | bytes 1048608 | tf_op jit(solution)/shard_map/ppermute | solution.py:264
  123.8 4.4 %shard_map.56.kv_ref.k_ref.v_ref = bf16[512,512]{1,0:T(8,128)(2,1)} custom-call(s32[1]{0:T(128)} %bitcast.2.base_ref, bf16[512,4096]{1,0:T(8,128)(2,1)} %pad_maximum_fusion.refs_0_.refs_1_.refs_2_.refs_3_, bf16[512,4096]{1,0:T(8,128)(2,1)} %pad_maximum_fusion.refs_0_.refs_1_.refs_2_.refs_3_, ...), custom_call_target="tpu_custom_call" | custom-call | tf_op jit(solution)/shard_map/pallas_call | solution.py:201
  132.0 34.6 %collective-permute-done.11 = bf16[2,128,128]{2,1,0:T(8,128)(2,1)S(1)} collective-permute-done((bf16[2,128,128]{2,1,0:T(8,128)(2,1)}, bf16[2,128,128]{2,1,0:T(8,128)(2,1)S(1)}, u32[]{:S(2)}, u32[]{:S(2)}) %collective-permute-start.11) | collective-permute-done | bytes 65568 | tf_op jit(solution)/shard_map/ppermute | solution.py:264
  169.6 3.6 %broadcast_select_fusion = (bf16[2048,512]{1,0:T(8,128)(2,1)}, bf16[2048,512]{1,0:T(8,128)(2,1)S(1)}) fusion(bf16[2048,512]{1,0:T(8,128)(2,1)} %constant_dynamic-update-slice_fusion.4, pred[]{:T(512)S(6)} %eq.47, bf16[512,512]{1,0:T(8,128)(2,1)} %copy-done.8, bf16[512,512]{1,0:T(8,128)(2,1)} %copy-done.6, bf16[512,512]{1,0:T(8,128)(2,1)} %copy-done.7, ...), kind=kLoop, calls=%fused_computation.4 | loop fusion | flops 10485760 | bytes 8388609 | tf_op jit(solution)/shard_map/jit(_where)/select_n | solution.py:334
  173.4 17.3 %collective-permute-done.12 = bf16[2,128,128]{2,1,0:T(8,128)(2,1)S(1)} collective-permute-done((bf16[2,128,128]{2,1,0:T(8,128)(2,1)S(1)}, bf16[2,128,128]{2,1,0:T(8,128)(2,1)S(1)}, u32[]{:S(2)}, u32[]{:S(2)}) %collective-permute-start.12) | collective-permute-done | bytes 65568 | tf_op jit(solution)/shard_map/ppermute | solution.py:264
  200.9 4.9 %shard_map.58.g_ref = bf16[512,1024]{1,0:T(8,128)(2,1)} custom-call(bf16[512,512]{1,0:T(8,128)(2,1)} %shard_map.56.kv_ref.k_ref.v_ref, bf16[512,512]{1,0:T(8,128)(2,1)} %shard_map.56.kv_ref.k_ref.v_ref, bf16[512,1024]{1,0:T(8,128)(2,1)} %pad_maximum_fusion.2.do_ref.refs_5_, bf16[2,2,128,128]{3,2,1,0:T(8,128)(2,1)} %pad_maximum_fusion.5.prefix_ref), custom_call_target="tpu_custom_call" | custom-call | tf_op jit(solution)/shard_map/pallas_call | solution.py:363
  205.8 12.7 %shard_map.59 = (f32[2,256,1536]{2,1,0:T(8,128)}, bf16[2,256,1536]{2,1,0:T(8,128)(2,1)}) custom-call(s32[1]{0:T(128)} %bitcast.1.side_ref, bf16[512,1024]{1,0:T(8,128)(2,1)} %shard_map.58.g_ref, bf16[512,1024]{1,0:T(8,128)(2,1)} %copy-done, bf16[512,1024]{1,0:T(8,128)(2,1)} %collective-permute-done.15.refs_1_.refs_5_, ...), custom_call_target="tpu_custom_call" | custom-call | tf_op jit(solution)/shard_map/pallas_call | solution.py:241
  219.1 6.5 %shard_map.61.refs_4_ = f32[512,1024]{1,0:T(8,128)} custom-call(s32[1]{0:T(128)} %bitcast.2.base_ref, bf16[512,4096]{1,0:T(8,128)(2,1)} %pad_maximum_fusion.refs_0_.refs_1_.refs_2_.refs_3_, bf16[512,4096]{1,0:T(8,128)(2,1)} %pad_maximum_fusion.refs_0_.refs_1_.refs_2_.refs_3_, bf16[512,4096]{1,0:T(8,128)(2,1)} %pad_maximum_fusion.refs_0_.refs_1_.refs_2_.refs_3_, ...), custom_call_target="tpu_custom_call" | custom-call | tf_op jit(solution)/shard_map/pallas_call | solution.py:201
  225.6 5.5 %shard_map.62.refs_4_ = f32[512,1024]{1,0:T(8,128)} custom-call(s32[1]{0:T(128)} %bitcast.2.base_ref, bf16[512,4096]{1,0:T(8,128)(2,1)} %pad_maximum_fusion.refs_0_.refs_1_.refs_2_.refs_3_, bf16[512,4096]{1,0:T(8,128)(2,1)} %pad_maximum_fusion.refs_0_.refs_1_.refs_2_.refs_3_, bf16[512,1024]{1,0:T(8,128)(2,1)} %collective-permute-done.18.refs_4_.refs_2_, ...), custom_call_target="tpu_custom_call" | custom-call | tf_op jit(solution)/shard_map/pallas_call | solution.py:201
  233.1 4.8 %shard_map.63 = (bf16[512,1024]{1,0:T(8,128)(2,1)}, bf16[2,2,128,128]{3,2,1,0:T(8,128)(2,1)}, bf16[2,128,128]{2,1,0:T(8,128)(2,1)}) custom-call(s32[1]{0:T(128)} %bitcast.2.base_ref, bf16[512,4096]{1,0:T(8,128)(2,1)} %pad_maximum_fusion.refs_0_.refs_1_.refs_2_.refs_3_, bf16[512,4096]{1,0:T(8,128)(2,1)} %pad_maximum_fusion.refs_0_.refs_1_.refs_2_.refs_3_, ...), custom_call_target="tpu_custom_call" | custom-call | tf_op jit(solution)/shard_map/pallas_call | solution.py:201
  252.2 3.6 %shard_map.65.refs_1_ = f32[512,256]{1,0:T(8,128)} custom-call(bf16[512,1024]{1,0:T(8,128)(2,1)} %get-tuple-element.24.q_ref, bf16[512,512]{1,0:T(8,128)(2,1)} %shard_map.56.kv_ref.k_ref.v_ref, bf16[512,512]{1,0:T(8,128)(2,1)} %shard_map.56.kv_ref.k_ref.v_ref, bf16[512,1024]{1,0:T(8,128)(2,1)} %pad_maximum_fusion.2.do_ref.refs_5_), custom_call_target="tpu_custom_call" | custom-call | tf_op jit(solution)/shard_map/pallas_call | solution.py:391
  255.7 3.6 %shard_map.64.refs_0_ = f32[512,256]{1,0:T(8,128)} custom-call(bf16[512,1024]{1,0:T(8,128)(2,1)} %get-tuple-element.24.q_ref, bf16[512,512]{1,0:T(8,128)(2,1)} %shard_map.56.kv_ref.k_ref.v_ref, bf16[512,512]{1,0:T(8,128)(2,1)} %shard_map.56.kv_ref.k_ref.v_ref, bf16[512,1024]{1,0:T(8,128)(2,1)} %pad_maximum_fusion.2.do_ref.refs_5_), custom_call_target="tpu_custom_call" | custom-call | tf_op jit(solution)/shard_map/pallas_call | solution.py:391
  262.5 5.2 %shard_map.60 = (f32[2,256,512]{2,1,0:T(8,128)}, bf16[2,256,512]{2,1,0:T(8,128)(2,1)}) custom-call(s32[1]{0:T(128)} %bitcast.1.side_ref, bf16[512,1024]{1,0:T(8,128)(2,1)} %shard_map.58.g_ref, bf16[512,1024]{1,0:T(8,128)(2,1)} %collective-permute-done.22.refs_0_.refs_2_, bf16[512,1024]{1,0:T(8,128)(2,1)} %copy-done.2), custom_call_target="tpu_custom_call" | custom-call | tf_op jit(solution)/shard_map/pallas_call | solution.py:241
  275.1 29.6 %collective-permute-done.26 = bf16[256,512]{1,0:T(8,128)(2,1)S(1)} collective-permute-done((bf16[256,512]{1,0:T(8,128)(2,1)S(1)}, bf16[256,512]{1,0:T(8,128)(2,1)S(1)}, u32[]{:S(2)}, u32[]{:S(2)}) %collective-permute-start.26) | collective-permute-done | bytes 262176 | tf_op jit(solution)/shard_map/ppermute | solution.py:267
  308.4 5.5 %shard_map.67 = bf16[256,2048]{1,0:T(8,128)(2,1)} custom-call(s32[1]{0:T(128)} %bitcast.base_ref, f32[256,2048]{1,0:T(8,128)} %fusion.sum_ref, bf16[256,1024]{1,0:T(8,128)(2,1)} %collective-permute-done.32.g_ref, bf16[2048,512]{1,0:T(8,128)(2,1)} %collective-permute-done.33.w_ref, bf16[2048,512]{1,0:T(8,128)(2,1)} %collective-permute-done.34.w_other_ref), custom_call_target="tpu_custom_call" | custom-call | tf_op jit(solution)/shard_map/pallas_call | solution.py:422
  (135 shorter events, 75.7 us)
Async XLA Ops:
  0.0 26.4 %collective-permute-start = (bf16[256,2048]{1,0:T(8,128)(2,1)}, bf16[256,2048]{1,0:T(8,128)(2,1)S(1)}, u32[]{:S(2)}, u32[]{:S(2)}) collective-permute-start(bf16[256,2048]{1,0:T(8,128)(2,1)} %param.5), channel_id=1, source_target_pairs={{0,1},{1,0},{2,3},{3,2},{4,5},{5,4},{6,7},{7,6},{8,9},{9,8},{10,11... | collective-permute-start | bytes 3145736 | tf_op jit(solution)/shard_map/ppermute | solution.py:267
  27.4 69.5 %collective-permute-start.1 = (bf16[256,4096]{1,0:T(8,128)(2,1)}, bf16[256,4096]{1,0:T(8,128)(2,1)}, u32[]{:S(2)}, u32[]{:S(2)}) collective-permute-start(bf16[256,4096]{1,0:T(8,128)(2,1)} %constant_dynamic-update-slice_fusion), channel_id=1, source_target_pairs={{0,2},{2,0},{4,6},{6,4},{8,10},{10,8},{12,14},{14,12},{16,18},{18,... | collective-permute-start | bytes 6291464 | tf_op jit(solution)/shard_map/ppermute | solution.py:264
  32.2 26.3 %collective-permute-start.5 = (bf16[512,512]{1,0:T(8,128)(2,1)S(1)}, bf16[512,512]{1,0:T(8,128)(2,1)S(1)}, u32[]{:S(2)}, u32[]{:S(2)}) collective-permute-start(bf16[512,512]{1,0:T(8,128)(2,1)S(1)} %constant_dynamic-update-slice_fusion.9.refs_4_), channel_id=1, source_target_pairs={{0,16},{2,18},{4,20},{6,22},{8,24},{10,26},{12,28},{14,30},{16,0},... | collective-permute-start | bytes 1572872 | tf_op jit(solution)/shard_map/ppermute | solution.py:264
  36.1 26.0 %collective-permute-start.14 = (bf16[256,1024]{1,0:T(8,128)(2,1)}, bf16[256,1024]{1,0:T(8,128)(2,1)}, u32[]{:S(2)}, u32[]{:S(2)}) collective-permute-start(bf16[256,1024]{1,0:T(8,128)(2,1)} %get-tuple-element.31), channel_id=1, source_target_pairs={{0,2},{2,0},{4,6},{6,4},{8,10},{10,8},{12,14},{14,12},{16,18},{18,... | collective-permute-start | bytes 1572872 | tf_op jit(solution)/shard_map/ppermute | solution.py:264
  60.1 27.4 %collective-permute-start.7 = (bf16[512,512]{1,0:T(8,128)(2,1)S(1)}, bf16[512,512]{1,0:T(8,128)(2,1)}, u32[]{:S(2)}, u32[]{:S(2)}) collective-permute-start(bf16[512,512]{1,0:T(8,128)(2,1)S(1)} %collective-permute-done.5.refs_7_), channel_id=1, source_target_pairs={{0,8},{2,10},{4,12},{6,14},{8,0},{10,2},{12,4},{14,6},{16,24},{18,... | collective-permute-start | bytes 1572872 | tf_op jit(solution)/shard_map/ppermute | solution.py:264
  60.8 36.1 %collective-permute-start.3 = (bf16[512,512]{1,0:T(8,128)(2,1)S(1)}, bf16[512,512]{1,0:T(8,128)(2,1)S(1)}, u32[]{:S(2)}, u32[]{:S(2)}) collective-permute-start(bf16[512,512]{1,0:T(8,128)(2,1)S(1)} %constant_dynamic-update-slice_fusion.9.refs_4_), channel_id=1, source_target_pairs={{0,8},{2,10},{4,12},{6,14},{8,0},{10,2},{12,4},{14,6},{16,24},{18,... | collective-permute-start | bytes 1572872 | tf_op jit(solution)/shard_map/ppermute | solution.py:264
  62.1 34.7 %collective-permute-start.9 = (bf16[512,512]{1,0:T(8,128)(2,1)S(1)}, bf16[512,512]{1,0:T(8,128)(2,1)S(1)}, u32[]{:S(2)}, u32[]{:S(2)}) collective-permute-start(bf16[512,512]{1,0:T(8,128)(2,1)S(1)} %constant_dynamic-update-slice_fusion.9.refs_4_), channel_id=1, source_target_pairs={{0,4},{2,6},{4,0},{6,2},{8,12},{10,14},{12,8},{14,10},{16,20},{18,... | collective-permute-start | bytes 1572872 | tf_op jit(solution)/shard_map/ppermute | solution.py:264
  73.4 45.8 %collective-permute-start.17 = (bf16[512,1024]{1,0:T(8,128)(2,1)S(1)}, bf16[512,1024]{1,0:T(8,128)(2,1)}, u32[]{:S(2)}, u32[]{:S(2)}) collective-permute-start(bf16[512,1024]{1,0:T(8,128)(2,1)S(1)} %constant_dynamic-update-slice_fusion.8.refs_0_.refs_4_), channel_id=1, source_target_pairs={{0,16},{2,18},{4,20},{6,22},{8,24},{10,26},{12,28},{14,30},{16,0},... | collective-permute-start | bytes 3145736 | tf_op jit(solution)/shard_map/ppermute | solution.py:264
  87.5 81.8 %collective-permute-start.10 = (bf16[256,1024]{1,0:T(8,128)(2,1)}, bf16[256,1024]{1,0:T(8,128)(2,1)}, u32[]{:S(2)}, u32[]{:S(2)}) collective-permute-start(bf16[256,1024]{1,0:T(8,128)(2,1)} %get-tuple-element.30), channel_id=1, source_target_pairs={{0,2},{2,0},{4,6},{6,4},{8,10},{10,8},{12,14},{14,12},{16,18},{18,... | collective-permute-start | bytes 1572872 | tf_op jit(solution)/shard_map/ppermute | solution.py:264
  96.8 76.3 %collective-permute-start.16 = (bf16[512,1024]{1,0:T(8,128)(2,1)S(1)}, bf16[512,1024]{1,0:T(8,128)(2,1)}, u32[]{:S(2)}, u32[]{:S(2)}) collective-permute-start(bf16[512,1024]{1,0:T(8,128)(2,1)S(1)} %constant_dynamic-update-slice_fusion.8.refs_0_.refs_4_), channel_id=1, source_target_pairs={{0,8},{2,10},{4,12},{6,14},{8,0},{10,2},{12,4},{14,6},{16,24},{18,... | collective-permute-start | bytes 3145736 | tf_op jit(solution)/shard_map/ppermute | solution.py:264
  97.0 26.0 %collective-permute-start.8 = (bf16[512,512]{1,0:T(8,128)(2,1)}, bf16[512,512]{1,0:T(8,128)(2,1)S(1)}, u32[]{:S(2)}, u32[]{:S(2)}) collective-permute-start(bf16[512,512]{1,0:T(8,128)(2,1)} %collective-permute-done.7.refs_6_), channel_id=1, source_target_pairs={{0,4},{2,6},{4,0},{6,2},{8,12},{10,14},{12,8},{14,10},{16,20},{18,... | collective-permute-start | bytes 1572872 | tf_op jit(solution)/shard_map/ppermute | solution.py:264
  111.7 94.1 %collective-permute-start.15 = (bf16[512,1024]{1,0:T(8,128)(2,1)S(1)}, bf16[512,1024]{1,0:T(8,128)(2,1)}, u32[]{:S(2)}, u32[]{:S(2)}) collective-permute-start(bf16[512,1024]{1,0:T(8,128)(2,1)S(1)} %constant_dynamic-update-slice_fusion.8.refs_0_.refs_4_), channel_id=1, source_target_pairs={{0,4},{2,6},{4,0},{6,2},{8,12},{10,14},{12,8},{14,10},{16,20},{18,... | collective-permute-start | bytes 3145736 | tf_op jit(solution)/shard_map/ppermute | solution.py:264
  119.2 77.9 %collective-permute-start.18 = (bf16[512,1024]{1,0:T(8,128)(2,1)}, bf16[512,1024]{1,0:T(8,128)(2,1)}, u32[]{:S(2)}, u32[]{:S(2)}) collective-permute-start(bf16[512,1024]{1,0:T(8,128)(2,1)} %collective-permute-done.17.refs_3_.refs_7_), channel_id=1, source_target_pairs={{0,4},{2,6},{4,0},{6,2},{8,12},{10,14},{12,8},{14,10},{16,20},{18,... | collective-permute-start | bytes 3145736 | tf_op jit(solution)/shard_map/ppermute | solution.py:264
  130.1 36.5 %collective-permute-start.11 = (bf16[2,128,128]{2,1,0:T(8,128)(2,1)}, bf16[2,128,128]{2,1,0:T(8,128)(2,1)S(1)}, u32[]{:S(2)}, u32[]{:S(2)}) collective-permute-start(bf16[2,128,128]{2,1,0:T(8,128)(2,1)} %get-tuple-element.16), channel_id=1, source_target_pairs={{0,4},{2,6},{4,0},{6,2},{8,12},{10,14},{12,8},{14,10},{16,20},{18,... | collective-permute-start | bytes 196616 | tf_op jit(solution)/shard_map/ppermute | solution.py:264
  166.6 26.0 %collective-permute-start.19 = (bf16[512,1024]{1,0:T(8,128)(2,1)}, bf16[512,1024]{1,0:T(8,128)(2,1)S(1)}, u32[]{:S(2)}, u32[]{:S(2)}) collective-permute-start(bf16[512,1024]{1,0:T(8,128)(2,1)} %collective-permute-done.17.refs_3_.refs_7_), channel_id=1, source_target_pairs={{0,8},{2,10},{4,12},{6,14},{8,0},{10,2},{12,4},{14,6},{16,24},{18,... | collective-permute-start | bytes 3145736 | tf_op jit(solution)/shard_map/ppermute | solution.py:264
  173.2 59.0 %collective-permute-start.22 = (bf16[512,1024]{1,0:T(8,128)(2,1)}, bf16[512,1024]{1,0:T(8,128)(2,1)}, u32[]{:S(2)}, u32[]{:S(2)}) collective-permute-start(bf16[512,1024]{1,0:T(8,128)(2,1)} %collective-permute-done.16.refs_2_.refs_6_), channel_id=1, source_target_pairs={{0,4},{2,6},{4,0},{6,2},{8,12},{10,14},{12,8},{14,10},{16,20},{18,... | collective-permute-start | bytes 3145736 | tf_op jit(solution)/shard_map/ppermute | solution.py:264
  190.8 77.7 %collective-permute-start.33 = (bf16[2048,512]{1,0:T(8,128)(2,1)}, bf16[2048,512]{1,0:T(8,128)(2,1)}, u32[]{:S(2)}, u32[]{:S(2)}) collective-permute-start(bf16[2048,512]{1,0:T(8,128)(2,1)} %get-tuple-element.27), channel_id=1, source_target_pairs={{0,1},{1,0},{2,3},{3,2},{4,5},{5,4},{6,7},{7,6},{8,9},{9,8},{10,11... | collective-permute-start | bytes 6291464 | tf_op jit(solution)/shard_map/ppermute | solution.py:267
  199.6 31.4 %collective-permute-start.24 = (bf16[320,1024]{1,0:T(8,128)(2,1)}, bf16[320,1024]{1,0:T(8,128)(2,1)}, u32[]{:S(2)}, u32[]{:S(2)}) collective-permute-start(bf16[320,1024]{1,0:T(8,128)(2,1)} %slice.83), channel_id=1, source_target_pairs={{0,8},{2,10},{4,12},{6,14},{8,0},{10,2},{12,4},{14,6},{16,24},{18,... | collective-permute-start | bytes 1966088 | tf_op jit(solution)/shard_map/ppermute | solution.py:264
  218.5 50.0 %collective-permute-start.20 = (bf16[2,256,1536]{2,1,0:T(8,128)(2,1)}, bf16[2,256,1536]{2,1,0:T(8,128)(2,1)}, u32[]{:S(2)}, u32[]{:S(2)}) collective-permute-start(bf16[2,256,1536]{2,1,0:T(8,128)(2,1)} %get-tuple-element.19), channel_id=1, source_target_pairs={{0,2},{2,0},{4,6},{6,4},{8,10},{10,8},{12,14},{14,12},{16,18},{18,... | collective-permute-start | bytes 4718600 | tf_op jit(solution)/shard_map/ppermute | solution.py:264
  218.5 54.0 %collective-permute-start.31 = (bf16[2048,512]{1,0:T(8,128)(2,1)S(1)}, bf16[2048,512]{1,0:T(8,128)(2,1)}, u32[]{:S(2)}, u32[]{:S(2)}) collective-permute-start(bf16[2048,512]{1,0:T(8,128)(2,1)S(1)} %get-tuple-element.28), channel_id=1, source_target_pairs={{0,2},{2,0},{4,6},{6,4},{8,10},{10,8},{12,14},{14,12},{16,18},{18,... | collective-permute-start | bytes 6291464 | tf_op jit(solution)/shard_map/ppermute | solution.py:264
  268.2 40.2 %collective-permute-start.32 = (bf16[256,1024]{1,0:T(8,128)(2,1)S(1)}, bf16[256,1024]{1,0:T(8,128)(2,1)}, u32[]{:S(2)}, u32[]{:S(2)}) collective-permute-start(bf16[256,1024]{1,0:T(8,128)(2,1)S(1)} %pad_maximum_fusion.3), channel_id=1, source_target_pairs={{0,1},{1,0},{2,3},{3,2},{4,5},{5,4},{6,7},{7,6},{8,9},{9,8},{10,11... | collective-permute-start | bytes 1572872 | tf_op jit(solution)/shard_map/ppermute | solution.py:267
  268.5 39.9 %collective-permute-start.34 = (bf16[2048,512]{1,0:T(8,128)(2,1)}, bf16[2048,512]{1,0:T(8,128)(2,1)}, u32[]{:S(2)}, u32[]{:S(2)}) collective-permute-start(bf16[2048,512]{1,0:T(8,128)(2,1)} %collective-permute-done.33.w_ref), channel_id=1, source_target_pairs={{0,2},{2,0},{4,6},{6,4},{8,10},{10,8},{12,14},{14,12},{16,18},{18,... | collective-permute-start | bytes 6291464 | tf_op jit(solution)/shard_map/ppermute | solution.py:264
  270.3 34.5 %collective-permute-start.21 = (bf16[256,1536]{1,0:T(8,128)(2,1)S(1)}, bf16[256,1536]{1,0:T(8,128)(2,1)S(1)}, u32[]{:S(2)}, u32[]{:S(2)}) collective-permute-start(bf16[256,1536]{1,0:T(8,128)(2,1)S(1)} %fusion.1), channel_id=1, source_target_pairs={{0,1},{1,0},{2,3},{3,2},{4,5},{5,4},{6,7},{7,6},{8,9},{9,8},{10,11... | collective-permute-start | bytes 2359304 | tf_op jit(solution)/shard_map/ppermute | solution.py:267
  272.3 32.4 %collective-permute-start.26 = (bf16[256,512]{1,0:T(8,128)(2,1)S(1)}, bf16[256,512]{1,0:T(8,128)(2,1)S(1)}, u32[]{:S(2)}, u32[]{:S(2)}) collective-permute-start(bf16[256,512]{1,0:T(8,128)(2,1)S(1)} %fusion.2), channel_id=1, source_target_pairs={{0,1},{1,0},{2,3},{3,2},{4,5},{5,4},{6,7},{7,6},{8,9},{9,8},{10,11... | collective-permute-start | bytes 786440 | tf_op jit(solution)/shard_map/ppermute | solution.py:267
  (31 other events, 406.0 us)

commit v2 on v1

--- a/solution.py
+++ b/solution.py
@@ -82,12 +82,6 @@
 NN, NT, TN = ((1,), (0,)), ((1,), (1,)), ((0,), (0,))
 
 
-def causal_mask(n):
-    return lax.broadcasted_iota(jnp.int32, (n, n), 0) >= lax.broadcasted_iota(
-        jnp.int32, (n, n), 1
-    )
-
-
 def head_cols(h):
     return slice(h * HEAD_DIM, (h + 1) * HEAD_DIM)
 
@@ -105,9 +99,16 @@
         total_ref[g] = total.astype(BF16)
 
 
+def scores_mask(n):
+    return lax.broadcasted_iota(jnp.int32, (n, n), 0) <= lax.broadcasted_iota(
+        jnp.int32, (n, n), 1
+    )
+
+
 def grad_query_kernel(k_ref, v_ref, do_ref, prefix_ref, out_ref):
     k, v, prefix = k_ref[...], v_ref[...], prefix_ref[0, 0]
-    mask = causal_mask(k.shape[0])
+    shape = (k.shape[0], k.shape[0])
+    mask = lax.broadcasted_iota(jnp.int32, shape, 0) >= lax.broadcasted_iota(jnp.int32, shape, 1)
     for h in range(GROUP):
         do = do_ref[:, head_cols(h)]
         ds = jnp.where(mask, mm(do, v, NT), 0.0).astype(BF16)
@@ -116,8 +117,7 @@
 
 def inner_kernel(q_ref, k_ref, v_ref, do_ref, out_ref):
     k, v = k_ref[...], v_ref[...]
-    shape = (k.shape[0], k.shape[0])
-    mask = lax.broadcasted_iota(jnp.int32, shape, 0) <= lax.broadcasted_iota(jnp.int32, shape, 1)
+    mask = scores_mask(k.shape[0])
     gk = jnp.zeros(k.shape, F32)
     gv = jnp.zeros(k.shape, F32)
     for h in range(GROUP):
@@ -149,19 +149,24 @@
 
 def project_call(base, x, weights, total, dtype, do=None):
     slots = sorted(weights)
-    rows, cols = weights[slots[0]].shape
+    pieces = [weights[i] if isinstance(weights[i], tuple) else (weights[i],) for i in slots]
+    cols = pieces[0][0].shape[1]
+    rows = sum(w.shape[0] for w in pieces[0])
     tokens = x.shape[0] // 2
     width = GROUP * HEAD_DIM if do is not None else rows // 2
     n = len(slots)
 
     def body(base_ref, *refs):
-        xs, ws = refs[:n], refs[n : 2 * n]
-        rest = list(refs[2 * n :])
+        xs, rest = refs[:n], list(refs[n:])
+        ws = [[rest.pop(0) for _ in piece] for piece in pieces]
         acc = rest.pop(0)[...] if total is not None else None
         do_ref = rest.pop(0) if do is not None else None
-        for x_ref, w_ref in zip(xs, ws):
-            part = mm(x_ref[...], w_ref[...], NN)
-            acc = part if acc is None else acc + part
+        for x_ref, w_refs in zip(xs, ws):
+            at = 0
+            for w_ref in w_refs:
+                part = mm(x_ref[:, at : at + w_ref.shape[0]], w_ref[...], NN)
+                acc = part if acc is None else acc + part
+                at += w_ref.shape[0]
         acc = acc.astype(dtype)
         rest[0][...] = acc
         if do_ref is not None:
@@ -182,9 +187,11 @@
         return pl.BlockSpec((2 * tokens, rows), lambda j, b: (0, b[0] ^ i))
 
     tile = pl.BlockSpec((2 * tokens, width), lambda j, b: (0, j))
-    args = [x] * n + [weights[i] for i in slots]
+    args = [x] * n + [w for piece in pieces for w in piece]
     in_specs = [x_spec(i) for i in slots]
-    in_specs += [pl.BlockSpec((rows, width), lambda j, b: (0, j))] * n
+    in_specs += [
+        pl.BlockSpec((w.shape[0], width), lambda j, b: (0, j)) for piece in pieces for w in piece
+    ]
     out_shape, out_specs = [jax.ShapeDtypeStruct((2 * tokens, cols), dtype)], [tile]
     if total is not None:
         args.append(total)
@@ -212,49 +219,62 @@
 
 
 def back_call(side, grads, low, high):
-    weights = low + high
     n = len(low)
-    rows, inner = weights[0].shape
+    pieces = [w if isinstance(w, tuple) else (w,) for w in low + high]
+    rows = sum(w.shape[0] for w in pieces[0])
+    inner = grads.shape[1]
     tokens = grads.shape[0] // 2
     half = rows // 2
 
     def body(side_ref, g_ref, *refs):
-        ws, (keep_ref, send_ref) = refs[:-2], refs[-2:]
-        for m, w_ref in enumerate(ws):
-
-            @pl.when(pl.program_id(0) == m)
-            def _():
-                both = mm(g_ref[...], w_ref[...], NT)
-                keep_ref[0] = both[:tokens]
-                send_ref[0] = both[tokens:].astype(BF16)
-
-    def w_spec(m):
-        return pl.BlockSpec(
-            (half, inner),
-            lambda i, j, b: (jnp.where(i == m, j, jnp.where(i < m, 0, 1)), 0),
-        )
-
-    out = pl.BlockSpec(
-        (1, tokens, half), lambda i, j, b: ((i // n) ^ b[0], 0, (i % n) * 2 + j)
-    )
-    shape = (2, tokens, n * rows)
+        rest, (keep_ref, send_ref) = list(refs[:-2]), refs[-2:]
+        first = pl.program_id(0) == 0
+        for m, piece in enumerate(pieces):
+            w = [rest.pop(0)[...] for _ in piece]
+            if len(w) > 1:
+                w = jnp.concatenate(w, 0)
+                w = jnp.where(first, w[:half], w[half:])
+            else:
+                w = w[0]
+            both = mm(g_ref[...], w, NT)
+            where = side_ref[0] if m < n else 1 - side_ref[0]
+            keep_ref[where, m % n] = both[:tokens]
+            send_ref[where, m % n] = both[tokens:].astype(BF16)
+
+    in_specs = [pl.BlockSpec(grads.shape, lambda j, b: (0, 0))]
+    for piece in pieces:
+        if len(piece) == 1:
+            in_specs.append(pl.BlockSpec((half, inner), lambda j, b: (j, 0)))
+        else:
+            in_specs += [pl.BlockSpec(w.shape, lambda j, b: (0, 0)) for w in piece]
+    out = pl.BlockSpec((2, n, tokens, half), lambda j, b: (0, 0, 0, j))
+    shape = (2, n, tokens, rows)
     return pl.pallas_call(
         body,
         out_shape=(jax.ShapeDtypeStruct(shape, F32), jax.ShapeDtypeStruct(shape, BF16)),
         grid_spec=pltpu.PrefetchScalarGridSpec(
-            num_scalar_prefetch=1,
-            grid=(2 * n, 2),
-            in_specs=[pl.BlockSpec(grads.shape, lambda i, j, b: (0, 0))]
-            + [w_spec(m) for m in range(2 * n)],
-            out_specs=(out, out),
+            num_scalar_prefetch=1, grid=(2,), in_specs=in_specs, out_specs=(out, out)
         ),
-    )(side, grads, *weights)
-
-
-def finish_kernel(base_ref, sum_ref, g_ref, w_ref, w_other_ref, out_ref):
-    n = w_ref.shape[1]
-    total = sum_ref[...] + mm(g_ref[:, :n], w_ref[...], NT)
-    out_ref[...] = (total + mm(g_ref[:, n:], w_other_ref[...], NT)).astype(BF16)
+    )(side, grads, *(w for piece in pieces for w in piece))
+
+
+def add_two(total, g, g_other, w, w_other):
+    return total + mm(g, w, NT) + mm(g_other, w_other, NT)
+
+
+def home_kernel(sum_ref, g_ref, g_other_ref, w_ref, w_other_ref, out_ref):
+    out_ref[0] = add_two(
+        sum_ref[0], g_ref[...], g_other_ref[...], w_ref[...], w_other_ref[...]
+    )
+
+
+def finish_kernel(base_ref, sum_ref, g_ref, g_other_ref, w_ref, w_other_ref, out_ref):
+    slots, _, width = sum_ref.shape
+    for i in range(slots):
+        at = base_ref[0] ^ i
+        out_ref[:, i * width : (i + 1) * width] = add_two(
+            sum_ref[at], g_ref[...], g_other_ref[...], w_ref[at], w_other_ref[at]
+        ).astype(BF16)
 
 
 def make_split(zs, xs, ys):
@@ -298,6 +318,9 @@
                 [w[:, head_cols(g)] for g in range(groups) for w in (k, v)], 1
             )
 
+        def gate(value, *first):
+            return lax.optimization_barrier((value,) + first)[0]
+
         def scalar(value):
             return value.reshape(1).astype(jnp.int32)
 
@@ -305,7 +328,7 @@
         chunk_b = in_order(cols(query_weight, core), cols(query_weight, 1 - core))
         do_all = own_and_other(cols(grad_out, core), cols(grad_out, 1 - core))
         acts = jnp.concatenate([activations, swap_y(activations)], 1)
-        acts = own_and_other(acts, acts)
+        acts = gate(own_and_other(acts, acts), do_all)
         base = scalar(side * per_half + chip % per_half)
 
         def project(weights, which, total, dtype, do=None):
@@ -315,7 +338,8 @@
 
         w_kv, w_q = [chunk_a] + [None] * (chips - 1), [chunk_b] + [None] * (chips - 1)
         w_kv[4], w_kv[2] = swap(chunk_a, Z2), swap(chunk_a, Z1)
-        w_kv[1], w_q[1] = swap(chunk_a, X1), swap(chunk_b, X1)
+        w_kv[1] = swap(chunk_a, X1)
+        w_q[1] = (swap(chunk_b[:tokens], X1), swap(chunk_b[tokens:], X1))
         w_kv[6] = swap(w_kv[4], Z1)
         w_q[4], w_q[2] = swap(chunk_b, Z2), swap(chunk_b, Z1)
         w_kv[3], w_kv[5] = swap(w_kv[2], X1), swap(w_kv[4], X1)
@@ -325,8 +349,8 @@
         kv = project(w_kv, (3, 5, 6, 7), kv_sum, BF16)
         w_q[3] = swap(w_q[2], X1)
         q_sum = project(w_q, (0, 1, 2, 4), None, F32)
-        cut = chunk_b.shape[0] * 3 // 8
-        w_q[7] = jnp.concatenate([swap(w_q[6][:cut], X1), swap(w_q[5][cut:], Z1)], 0)
+        cut = tokens // 2
+        w_q[7] = (swap(w_q[6][:cut], X1), swap(w_q[5][cut:], Z1))
 
         n_half = chips // ys
         low, high = jnp.concatenate(w_kv[:n_half], 0), jnp.concatenate(w_kv[n_half:], 0)
@@ -373,15 +397,18 @@
             out_specs=q_spec,
         )(kv, kv, do_all, prefix)
 
-        def back(which):
+        def back(which, after=None):
             keep, send = back_call(
                 scalar(side), gq, [w_q[i] for i in which], [w_q[i + n_half] for i in which]
             )
             got = swap(send, C1)
+            if after is not None:
+                keep = gate(keep, after)
             away = (keep[1] + got[1].astype(F32)).astype(BF16)
-            return keep[0], got[0], swap_y(away)
-
-        early = back(range(n_half - 1))
+            return keep[0], got[0], swap_y(away), away
+
+        sums = [back((0, 1))]
+        sums.append(back((2,), sums[0][3]))
         q_sum = project(w_q, (5, 6), q_sum, F32)
         q, gs, total = project(w_q, (3, 7), q_sum, BF16, do_all)
         outside, got, counts = scan(total, False)
@@ -401,7 +428,7 @@
                     out_specs=pl.BlockSpec((tokens, 2 * HEAD_DIM), lambda n: (n, 0)),
                 )(q, kv, kv, do_all)
             )
-        late = back((n_half - 1,))
+        sums.append(back((3,)))
         flags = jnp.stack([counts, core == 0]).astype(jnp.int32)
         part = jax.ShapeDtypeStruct((tokens, 2 * groups * HEAD_DIM), BF16)
         vmem = pl.BlockSpec(memory_space=pltpu.VMEM)
@@ -411,29 +438,35 @@
             in_specs=[pl.BlockSpec(memory_space=pltpu.SMEM)] + [vmem] * (4 + groups),
             out_specs=(vmem, vmem),
         )(flags, kv, outside, got, gs, *inner)
-        gkv_c = swap(gkv_other, C1)
-        far = swap_y(jnp.concatenate([gkv, gkv_c], 1))
+        far_other, far = swap_y(gkv_other), swap_y(gkv)
+        gkv_c, far_c = swap(gkv_other, C1), swap(far_other, C1)
         home = jnp.concatenate(
-            [p[0] + p[1].astype(F32) + p[2].astype(F32) for p in (early, late)], 1
-        )
-        home = home + mm(gkv, w_home, NT) + mm(gkv_c, w_home_c, NT)
-        width = home.shape[1] // n_half
-        w_spec = pl.BlockSpec((width, w_home.shape[1]), lambda i, b: (b[0] ^ i, 0))
+            [p[0] + p[1].astype(F32) + p[2].astype(F32) for p in sums], 0
+        )
+        slots, width = home.shape[0], home.shape[2]
+        home = pl.pallas_call(
+            home_kernel,
+            out_shape=jax.ShapeDtypeStruct(home.shape, F32),
+            grid=(slots,),
+            in_specs=[pl.BlockSpec((1, tokens, width), lambda i: (i, 0, 0))]
+            + [pl.BlockSpec(gkv.shape, lambda i: (0, 0))] * 2
+            + [pl.BlockSpec((width, w_home.shape[1]), lambda i: (i, 0))] * 2,
+            out_specs=pl.BlockSpec((1, tokens, width), lambda i: (i, 0, 0)),
+        )(home, gkv, gkv_c, w_home, w_home_c)
+        by_slot = (slots, width, w_home.shape[1])
         return pl.pallas_call(
             finish_kernel,
-            out_shape=jax.ShapeDtypeStruct(home.shape, BF16),
-            grid_spec=pltpu.PrefetchScalarGridSpec(
-                num_scalar_prefetch=1,
-                grid=(n_half,),
-                in_specs=[
-                    pl.BlockSpec((tokens, width), lambda i, b: (0, b[0] ^ i)),
-                    pl.BlockSpec(far.shape, lambda i, b: (0, 0)),
-                    w_spec,
-                    w_spec,
-                ],
-                out_specs=pl.BlockSpec((tokens, width), lambda i, b: (0, i)),
-            ),
-        )(scalar(chip % per_half), home, far, w_home_y, w_home_cy)
+            out_shape=jax.ShapeDtypeStruct((tokens, slots * width), BF16),
+            in_specs=[pl.BlockSpec(memory_space=pltpu.SMEM)] + [vmem] * 5,
+            out_specs=vmem,
+        )(
+            scalar(chip % per_half),
+            home,
+            far,
+            far_c,
+            w_home_y.reshape(by_slot),
+            w_home_cy.reshape(by_slot),
+        )
 
     return local
 

time: 315 us -> 281 us (0.89)
  waiting for transfers between devices: 177 us -> 121 us
  starting transfers between devices: 29.3 us -> 50.9 us
  other arithmetic: 18.6 us -> 26 us
  matrix products: 4.64 us -> 0 us
  local copies, waits for them, and re-layouts: 18.4 us -> 14.5 us
    ppermute x30 -> x33, waiting for transfers between devices: 126 us -> 80.6 us  [swap(): return lax.ppermute(value, 'seq', [(s, s ^ bit) for s in range(n_seq)])]
    ppermute x30 -> x33, starting transfers between devices: 22.1 us -> 37.5 us  [swap(): return lax.ppermute(value, 'seq', [(s, s ^ bit) for s in range(n_seq)])]
    ppermute x5 -> x7, waiting for transfers between devices: 50.6 us -> 40.1 us  [swap_y(): return lax.ppermute(value, 'head', [(y, y ^ 1) for y in range(ys)])]
    ppermute x5 -> x7, starting transfers between devices: 7.24 us -> 13.4 us  [swap_y(): return lax.ppermute(value, 'head', [(y, y ^ 1) for y in range(ys)])]
    pallas_call x1 -> x2, Pallas kernels: 5.52 us -> 11 us  [the longest x1 5.72 us: local(): pl.pallas_call(home_kernel, out_shape=jax.ShapeDtypeStruct(home.shape, F3...]
    dot_general x2 -> x0, matrix products: 4.64 us -> none  [mm(): lax.dot_general(a, b, (contract, ((), ())), preferred_element_type=F32)]
    pallas_call x2 -> x3, Pallas kernels: 17.9 us -> 14 us  [back_call(): pl.pallas_call(body, out_shape=(jax.ShapeDtypeStruct(shape, F32), jax.Sha...]
    unnamed x45 -> x50, local copies, waits for them, and re-layouts: 7.03 us -> 4.66 us
  transfers between devices with their start and end apart: 35 -> 40, of which waited for: 14 -> 14; matrix products, arithmetic and copies ran while one was open for 12% -> 14% of each run, Pallas kernels for 19% -> 22%
where the time goes in v2:
time: 281 us; the launch traced here: 280 us
  waiting for transfers between devices  121 us (43%)
  Pallas kernels  67.8 us (24%)
  starting transfers between devices  50.9 us (18%)
  other arithmetic  26 us (9%)
  local copies, waits for them, and re-layouts  14.5 us (5%)
    ppermute x33, waiting for transfers between devices, swap(): return lax.ppermute(value, 'seq', [(s, s ^ bit) for s in range(n_seq)])  80.6 us
    ppermute x7, waiting for transfers between devices, swap_y(): return lax.ppermute(value, 'head', [(y, y ^ 1) for y in range(ys)])  40.1 us
    ppermute x33, starting transfers between devices, swap(): return lax.ppermute(value, 'seq', [(s, s ^ bit) for s in range(n_seq)])  37.5 us
    pallas_call x5, Pallas kernels, project_call(): pl.pallas_call(body, out_shape=out_shape, grid_spec=pltpu.PrefetchScalarG...  26 us
    pallas_call x3, Pallas kernels, back_call(): pl.pallas_call(body, out_shape=(jax.ShapeDtypeStruct(shape, F32), jax.Sha...  14 us
    ppermute x7, starting transfers between devices, swap_y(): return lax.ppermute(value, 'head', [(y, y ^ 1) for y in range(ys)])  13.4 us
    pallas_call x2, Pallas kernels, local(): pl.pallas_call(inner_kernel, out_shape=jax.ShapeDtypeStruct((2 * tokens,...  7.44 us
    select_n x1, other arithmetic, local(): w_home_y = swap_y(jnp.where(side == 0, high, low))  6.65 us
  transfers between devices with their start and end apart: 40, of which 14 were waited for; matrix products, arithmetic and copies ran while one was open for 14% of the time, Pallas kernels for 22%

profile of v2, /device:TPU:0, one launch (start us, length us, event | category | flops | bytes accessed | tf_op | source)
XLA Modules:
  0.0 280.3 jit_solution(7826281042786619991)
XLA Ops:
  9.5 17.0 %collective-permute-done = bf16[256,2048]{1,0:T(8,128)(2,1)} collective-permute-done((bf16[256,2048]{1,0:T(8,128)(2,1)}, bf16[256,2048]{1,0:T(8,128)(2,1)}, u32[]{:S(2)}, u32[]{:S(2)}) %collective-permute-start) | collective-permute-done | bytes 1048608 | tf_op jit(solution)/shard_map/ppermute | solution.py:287
  38.9 23.3 %collective-permute-done.4.refs_6_ = bf16[512,512]{1,0:T(8,128)(2,1)S(1)} collective-permute-done((bf16[512,512]{1,0:T(8,128)(2,1)S(1)}, bf16[512,512]{1,0:T(8,128)(2,1)S(1)}, u32[]{:S(2)}, u32[]{:S(2)}) %collective-permute-start.4) | collective-permute-done | bytes 524320 | tf_op jit(solution)/shard_map/ppermute | solution.py:284
  65.0 8.2 %collective-permute-done.8.refs_6_ = bf16[512,512]{1,0:T(8,128)(2,1)} collective-permute-done((bf16[512,512]{1,0:T(8,128)(2,1)S(1)}, bf16[512,512]{1,0:T(8,128)(2,1)}, u32[]{:S(2)}, u32[]{:S(2)}) %collective-permute-start.8) | collective-permute-done | bytes 524320 | tf_op jit(solution)/shard_map/ppermute | solution.py:284
  78.1 20.7 %collective-permute-done.9.refs_7_ = bf16[512,512]{1,0:T(8,128)(2,1)S(1)} collective-permute-done((bf16[512,512]{1,0:T(8,128)(2,1)}, bf16[512,512]{1,0:T(8,128)(2,1)S(1)}, u32[]{:S(2)}, u32[]{:S(2)}) %collective-permute-start.9) | collective-permute-done | bytes 524320 | tf_op jit(solution)/shard_map/ppermute | solution.py:284
  101.3 6.7 %broadcast_select_fusion = (bf16[2048,512]{1,0:T(8,128)(2,1)}, bf16[2048,512]{1,0:T(8,128)(2,1)S(1)}) fusion(bf16[2048,512]{1,0:T(8,128)(2,1)S(1)} %constant_dynamic-update-slice_fusion.2, pred[]{:T(512)S(6)} %eq.47, bf16[512,512]{1,0:T(8,128)(2,1)S(1)} %collective-permute-done.5.refs_4_, bf16[512,512]{1,0:T(8,128)(2,1)} %copy-done.5, ...), kind=kLoop, calls=%fused_computation.3 | loop fusion | flops 10485760 | bytes 8388609 | tf_op jit(solution)/shard_map/jit(_where)/select_n | solution.py:358
  113.3 4.7 %pad_maximum_fusion.refs_0_.refs_1_.refs_2_.refs_3_ = bf16[512,4096]{1,0:T(8,128)(2,1)} fusion(bf16[256,4096]{1,0:T(8,128)(2,1)} %collective-permute-done.1, bf16[256,4096]{1,0:T(8,128)(2,1)} %constant_dynamic-update-slice_fusion), kind=kLoop, calls=%fused_computation | loop fusion | flops 8388608 | bytes 8388608 | tf_op jit(solution)/shard_map/concatenate | solution.py:306
  118.0 4.2 %shard_map.55.refs_8_ = f32[512,512]{1,0:T(8,128)} custom-call(s32[1]{0:T(128)} %bitcast.2.base_ref, bf16[512,4096]{1,0:T(8,128)(2,1)} %pad_maximum_fusion.refs_0_.refs_1_.refs_2_.refs_3_, bf16[512,4096]{1,0:T(8,128)(2,1)} %pad_maximum_fusion.refs_0_.refs_1_.refs_2_.refs_3_, bf16[512,4096]{1,0:T(8,128)(2,1)} %pad_maximum_fusion.refs_0_.refs_1_.refs_2_.refs_3_, ...), custom_call_target="tpu_custom_call" | custom-call | tf_op jit(solution)/shard_map/pallas_call | solution.py:208
  122.2 4.4 %shard_map.56.kv_ref.k_ref.v_ref = bf16[512,512]{1,0:T(8,128)(2,1)} custom-call(s32[1]{0:T(128)} %bitcast.2.base_ref, bf16[512,4096]{1,0:T(8,128)(2,1)} %pad_maximum_fusion.refs_0_.refs_1_.refs_2_.refs_3_, bf16[512,4096]{1,0:T(8,128)(2,1)} %pad_maximum_fusion.refs_0_.refs_1_.refs_2_.refs_3_, ...), custom_call_target="tpu_custom_call" | custom-call | tf_op jit(solution)/shard_map/pallas_call | solution.py:208
  130.3 7.1 %collective-permute-done.11 = bf16[2,128,128]{2,1,0:T(8,128)(2,1)S(1)} collective-permute-done((bf16[2,128,128]{2,1,0:T(8,128)(2,1)}, bf16[2,128,128]{2,1,0:T(8,128)(2,1)S(1)}, u32[]{:S(2)}, u32[]{:S(2)}) %collective-permute-start.11) | collective-permute-done | bytes 65568 | tf_op jit(solution)/shard_map/ppermute | solution.py:284
  144.2 4.6 %collective-permute-done.12 = bf16[2,128,128]{2,1,0:T(8,128)(2,1)S(1)} collective-permute-done((bf16[2,128,128]{2,1,0:T(8,128)(2,1)S(1)}, bf16[2,128,128]{2,1,0:T(8,128)(2,1)S(1)}, u32[]{:S(2)}, u32[]{:S(2)}) %collective-permute-start.12) | collective-permute-done | bytes 65568 | tf_op jit(solution)/shard_map/ppermute | solution.py:284
  154.3 10.1 %collective-permute-done.13 = bf16[2,128,128]{2,1,0:T(8,128)(2,1)} collective-permute-done((bf16[2,128,128]{2,1,0:T(8,128)(2,1)S(1)}, bf16[2,128,128]{2,1,0:T(8,128)(2,1)}, u32[]{:S(2)}, u32[]{:S(2)}) %collective-permute-start.13) | collective-permute-done | bytes 65568 | tf_op jit(solution)/shard_map/ppermute | solution.py:284
  167.8 4.8 %shard_map.58.g_ref = bf16[512,1024]{1,0:T(8,128)(2,1)} custom-call(bf16[512,512]{1,0:T(8,128)(2,1)} %shard_map.56.kv_ref.k_ref.v_ref, bf16[512,512]{1,0:T(8,128)(2,1)} %shard_map.56.kv_ref.k_ref.v_ref, bf16[512,1024]{1,0:T(8,128)(2,1)} %pad_maximum_fusion.3.do_ref.refs_6_, bf16[2,2,128,128]{3,2,1,0:T(8,128)(2,1)} %pad_maximum_fusion.5.prefix_ref), custom_call_target="tpu_custom_call" | custom-call | tf_op jit(solution)/shard_map/pallas_call | solution.py:387
  175.0 6.0 %shard_map.59 = (f32[2,2,256,512]{3,2,1,0:T(8,128)}, bf16[2,2,256,512]{3,2,1,0:T(8,128)(2,1)}) custom-call(s32[1]{0:T(128)} %bitcast.1.side_ref, bf16[512,1024]{1,0:T(8,128)(2,1)} %shard_map.58.g_ref, bf16[512,1024]{1,0:T(8,128)(2,1)} %copy-done, bf16[256,1024]{1,0:T(8,128)(2,1)} %collective-permute-done.15.refs_1_.refs_5_, ...), custom_call_target="tpu_custom_call" | custom-call | tf_op jit(solution)/shard_map/pallas_call | solution.py:252
  181.0 6.6 %shard_map.62.refs_4_ = f32[512,1024]{1,0:T(8,128)} custom-call(s32[1]{0:T(128)} %bitcast.2.base_ref, bf16[512,4096]{1,0:T(8,128)(2,1)} %pad_maximum_fusion.refs_0_.refs_1_.refs_2_.refs_3_, bf16[512,4096]{1,0:T(8,128)(2,1)} %pad_maximum_fusion.refs_0_.refs_1_.refs_2_.refs_3_, bf16[512,4096]{1,0:T(8,128)(2,1)} %pad_maximum_fusion.refs_0_.refs_1_.refs_2_.refs_3_, ...), custom_call_target="tpu_custom_call" | custom-call | tf_op jit(solution)/shard_map/pallas_call | solution.py:208
  187.6 5.5 %shard_map.63.refs_5_ = f32[512,1024]{1,0:T(8,128)} custom-call(s32[1]{0:T(128)} %bitcast.2.base_ref, bf16[512,4096]{1,0:T(8,128)(2,1)} %pad_maximum_fusion.refs_0_.refs_1_.refs_2_.refs_3_, bf16[512,4096]{1,0:T(8,128)(2,1)} %pad_maximum_fusion.refs_0_.refs_1_.refs_2_.refs_3_, bf16[512,1024]{1,0:T(8,128)(2,1)} %collective-permute-done.18.refs_4_.refs_2_, ...), custom_call_target="tpu_custom_call" | custom-call | tf_op jit(solution)/shard_map/pallas_call | solution.py:208
  194.1 5.3 %shard_map.64 = (bf16[512,1024]{1,0:T(8,128)(2,1)}, bf16[2,2,128,128]{3,2,1,0:T(8,128)(2,1)}, bf16[2,128,128]{2,1,0:T(8,128)(2,1)}) custom-call(s32[1]{0:T(128)} %bitcast.2.base_ref, bf16[512,4096]{1,0:T(8,128)(2,1)} %pad_maximum_fusion.refs_0_.refs_1_.refs_2_.refs_3_, bf16[512,4096]{1,0:T(8,128)(2,1)} %pad_maximum_fusion.refs_0_.refs_1_.refs_2_.refs_3_, ...), custom_call_target="tpu_custom_call" | custom-call | tf_op jit(solution)/shard_map/pallas_call | solution.py:208
  201.2 4.1 %shard_map.61 = (f32[2,1,256,512]{3,2,1,0:T(8,128)}, bf16[2,1,256,512]{3,2,1,0:T(8,128)(2,1)}) custom-call(s32[1]{0:T(128)} %bitcast.1.side_ref, bf16[512,1024]{1,0:T(8,128)(2,1)} %shard_map.58.g_ref, bf16[512,1024]{1,0:T(8,128)(2,1)} %copy-done.4, bf16[128,1024]{1,0:T(8,128)(2,1)} %copy-done.16, bf16[384,1024]{1,0:T(8,128)(2,1)} %collective-permute-done.27.refs_2_.refs_4_), custom_call_target="tpu_custom_call" | custom-call | tf_op jit(solution)/shard_map/pallas_call | solution.py:252
  214.0 4.0 %shard_map.60 = (f32[2,1,256,512]{3,2,1,0:T(8,128)}, bf16[2,1,256,512]{3,2,1,0:T(8,128)(2,1)}) custom-call(s32[1]{0:T(128)} %bitcast.1.side_ref, bf16[512,1024]{1,0:T(8,128)(2,1)} %shard_map.58.g_ref, bf16[512,1024]{1,0:T(8,128)(2,1)} %collective-permute-done.21.refs_0_.refs_7_, bf16[512,1024]{1,0:T(8,128)(2,1)} %collective-permute-done.22.refs_1_.refs_3_), custom_call_target="tpu_custom_call" | custom-call | tf_op jit(solution)/shard_map/pallas_call | solution.py:252
  221.6 3.9 %shard_map.66.refs_1_ = f32[512,256]{1,0:T(8,128)} custom-call(bf16[512,1024]{1,0:T(8,128)(2,1)} %get-tuple-element.32.q_ref, bf16[512,512]{1,0:T(8,128)(2,1)} %shard_map.56.kv_ref.k_ref.v_ref, bf16[512,512]{1,0:T(8,128)(2,1)} %shard_map.56.kv_ref.k_ref.v_ref, bf16[512,1024]{1,0:T(8,128)(2,1)} %pad_maximum_fusion.3.do_ref.refs_6_), custom_call_target="tpu_custom_call" | custom-call | tf_op jit(solution)/shard_map/pallas_call | solution.py:418
  235.2 4.3 %collective-permute-done.29 = bf16[1,256,512]{2,1,0:T(8,128)(2,1)S(1)} collective-permute-done((bf16[1,256,512]{2,1,0:T(8,128)(2,1)S(1)}, bf16[1,256,512]{2,1,0:T(8,128)(2,1)S(1)}, u32[]{:S(2)}, u32[]{:S(2)}) %collective-permute-start.29) | collective-permute-done | bytes 262176 | tf_op jit(solution)/shard_map/ppermute | solution.py:287
  242.6 13.5 %collective-permute-done.24 = bf16[1,256,512]{2,1,0:T(8,128)(2,1)S(1)} collective-permute-done((bf16[1,256,512]{2,1,0:T(8,128)(2,1)S(1)}, bf16[1,256,512]{2,1,0:T(8,128)(2,1)S(1)}, u32[]{:S(2)}, u32[]{:S(2)}) %collective-permute-start.24) | collective-permute-done | bytes 262176 | tf_op jit(solution)/shard_map/ppermute | solution.py:287
  258.9 5.3 %collective-permute-done.36 = bf16[256,512]{1,0:T(8,128)(2,1)S(1)} collective-permute-done((bf16[256,512]{1,0:T(8,128)(2,1)S(1)}, bf16[256,512]{1,0:T(8,128)(2,1)S(1)}, u32[]{:S(2)}, u32[]{:S(2)}) %collective-permute-start.36) | collective-permute-done | bytes 262176 | tf_op jit(solution)/shard_map/ppermute | solution.py:287
  268.5 5.7 %shard_map.68.sum_ref = f32[4,256,512]{2,1,0:T(8,128)} custom-call(f32[4,256,512]{2,1,0:T(8,128)} %pad_maximum_fusion.1.sum_ref, bf16[256,512]{1,0:T(8,128)(2,1)} %get-tuple-element.33.g_ref, bf16[256,512]{1,0:T(8,128)(2,1)} %collective-permute-done.33.g_other_ref, bf16[2048,512]{1,0:T(8,128)(2,1)} %copy-done.1, ...), custom_call_target="tpu_custom_call" | custom-call | tf_op jit(solution)/shard_map/pallas_call | solution.py:447
  275.1 5.3 %shard_map.69 = bf16[256,2048]{1,0:T(8,128)(2,1)} custom-call(s32[1]{0:T(128)} %bitcast.base_ref, f32[4,256,512]{2,1,0:T(8,128)} %shard_map.68.sum_ref, bf16[256,512]{1,0:T(8,128)(2,1)} %copy-done.18, bf16[256,512]{1,0:T(8,128)(2,1)} %copy-done.19, bf16[4,512,512]{2,1,0:T(8,128)(2,1)} %bitcast.15.w_ref, bf16[4,512,512]{2,1,0:T(8,128)(2,1)} %bitcast.16.w_other_ref), custom_call_target="tpu_custom_call" | custom-call | tf_op jit(solution)/shard_map/pallas_call | solution.py:457
  (152 shorter events, 94.8 us)
Async XLA Ops:
  0.0 26.5 %collective-permute-start = (bf16[256,2048]{1,0:T(8,128)(2,1)}, bf16[256,2048]{1,0:T(8,128)(2,1)}, u32[]{:S(2)}, u32[]{:S(2)}) collective-permute-start(bf16[256,2048]{1,0:T(8,128)(2,1)} %param.5), channel_id=1, source_target_pairs={{0,1},{1,0},{2,3},{3,2},{4,5},{5,4},{6,7},{7,6},{8,9},{9,8},{10,11... | collective-permute-start | bytes 3145736 | tf_op jit(solution)/shard_map/ppermute | solution.py:287
  4.5 29.6 %collective-permute-start.14 = (bf16[256,1024]{1,0:T(8,128)(2,1)S(1)}, bf16[256,1024]{1,0:T(8,128)(2,1)S(1)}, u32[]{:S(2)}, u32[]{:S(2)}) collective-permute-start(bf16[256,1024]{1,0:T(8,128)(2,1)S(1)} %get-tuple-element.39), channel_id=1, source_target_pairs={{0,2},{2,0},{4,6},{6,4},{8,10},{10,8},{12,14},{14,12},{16,18},{18,... | collective-permute-start | bytes 1572872 | tf_op jit(solution)/shard_map/ppermute | solution.py:284
  5.8 26.2 %collective-permute-start.6 = (bf16[512,512]{1,0:T(8,128)(2,1)S(1)}, bf16[512,512]{1,0:T(8,128)(2,1)S(1)}, u32[]{:S(2)}, u32[]{:S(2)}) collective-permute-start(bf16[512,512]{1,0:T(8,128)(2,1)S(1)} %constant_dynamic-update-slice_fusion.7.refs_4_), channel_id=1, source_target_pairs={{0,16},{2,18},{4,20},{6,22},{8,24},{10,26},{12,28},{14,30},{16,0},... | collective-permute-start | bytes 1572872 | tf_op jit(solution)/shard_map/ppermute | solution.py:284
  28.8 82.9 %collective-permute-start.1 = (bf16[256,4096]{1,0:T(8,128)(2,1)}, bf16[256,4096]{1,0:T(8,128)(2,1)}, u32[]{:S(2)}, u32[]{:S(2)}) collective-permute-start(bf16[256,4096]{1,0:T(8,128)(2,1)} %constant_dynamic-update-slice_fusion), channel_id=1, source_target_pairs={{0,2},{2,0},{4,6},{6,4},{8,10},{10,8},{12,14},{14,12},{16,18},{18,... | collective-permute-start | bytes 6291464 | tf_op jit(solution)/shard_map/ppermute | solution.py:284
  28.8 33.5 %collective-permute-start.4 = (bf16[512,512]{1,0:T(8,128)(2,1)S(1)}, bf16[512,512]{1,0:T(8,128)(2,1)S(1)}, u32[]{:S(2)}, u32[]{:S(2)}) collective-permute-start(bf16[512,512]{1,0:T(8,128)(2,1)S(1)} %constant_dynamic-update-slice_fusion.7.refs_4_), channel_id=1, source_target_pairs={{0,8},{2,10},{4,12},{6,14},{8,0},{10,2},{12,4},{14,6},{16,24},{18,... | collective-permute-start | bytes 1572872 | tf_op jit(solution)/shard_map/ppermute | solution.py:284
  32.0 33.0 %collective-permute-start.7 = (bf16[512,512]{1,0:T(8,128)(2,1)S(1)}, bf16[512,512]{1,0:T(8,128)(2,1)S(1)}, u32[]{:S(2)}, u32[]{:S(2)}) collective-permute-start(bf16[512,512]{1,0:T(8,128)(2,1)S(1)} %collective-permute-done.6.refs_7_), channel_id=1, source_target_pairs={{0,4},{2,6},{4,0},{6,2},{8,12},{10,14},{12,8},{14,10},{16,20},{18,... | collective-permute-start | bytes 1572872 | tf_op jit(solution)/shard_map/ppermute | solution.py:284
  33.4 39.8 %collective-permute-start.8 = (bf16[512,512]{1,0:T(8,128)(2,1)S(1)}, bf16[512,512]{1,0:T(8,128)(2,1)}, u32[]{:S(2)}, u32[]{:S(2)}) collective-permute-start(bf16[512,512]{1,0:T(8,128)(2,1)S(1)} %collective-permute-done.6.refs_7_), channel_id=1, source_target_pairs={{0,8},{2,10},{4,12},{6,14},{8,0},{10,2},{12,4},{14,6},{16,24},{18,... | collective-permute-start | bytes 1572872 | tf_op jit(solution)/shard_map/ppermute | solution.py:284
  34.2 66.6 %collective-permute-start.17 = (bf16[512,1024]{1,0:T(8,128)(2,1)S(1)}, bf16[512,1024]{1,0:T(8,128)(2,1)}, u32[]{:S(2)}, u32[]{:S(2)}) collective-permute-start(bf16[512,1024]{1,0:T(8,128)(2,1)S(1)} %constant_dynamic-update-slice_fusion.6.refs_0_.refs_4_), channel_id=1, source_target_pairs={{0,16},{2,18},{4,20},{6,22},{8,24},{10,26},{12,28},{14,30},{16,0},... | collective-permute-start | bytes 3145736 | tf_op jit(solution)/shard_map/ppermute | solution.py:284
  62.3 36.6 %collective-permute-start.10 = (bf16[512,512]{1,0:T(8,128)(2,1)S(1)}, bf16[512,512]{1,0:T(8,128)(2,1)S(1)}, u32[]{:S(2)}, u32[]{:S(2)}) collective-permute-start(bf16[512,512]{1,0:T(8,128)(2,1)S(1)} %constant_dynamic-update-slice_fusion.7.refs_4_), channel_id=1, source_target_pairs={{0,4},{2,6},{4,0},{6,2},{8,12},{10,14},{12,8},{14,10},{16,20},{18,... | collective-permute-start | bytes 1572872 | tf_op jit(solution)/shard_map/ppermute | solution.py:284
  64.9 34.0 %collective-permute-start.5 = (bf16[512,512]{1,0:T(8,128)(2,1)S(1)}, bf16[512,512]{1,0:T(8,128)(2,1)S(1)}, u32[]{:S(2)}, u32[]{:S(2)}) collective-permute-start(bf16[512,512]{1,0:T(8,128)(2,1)S(1)} %collective-permute-done.4.refs_6_), channel_id=1, source_target_pairs={{0,4},{2,6},{4,0},{6,2},{8,12},{10,14},{12,8},{14,10},{16,20},{18,... | collective-permute-start | bytes 1572872 | tf_op jit(solution)/shard_map/ppermute | solution.py:284
  98.8 29.7 %collective-permute-start.21 = (bf16[512,1024]{1,0:T(8,128)(2,1)S(1)}, bf16[512,1024]{1,0:T(8,128)(2,1)}, u32[]{:S(2)}, u32[]{:S(2)}) collective-permute-start(bf16[512,1024]{1,0:T(8,128)(2,1)S(1)} %constant_dynamic-update-slice_fusion.6.refs_0_.refs_4_), channel_id=1, source_target_pairs={{0,8},{2,10},{4,12},{6,14},{8,0},{10,2},{12,4},{14,6},{16,24},{18,... | collective-permute-start | bytes 3145736 | tf_op jit(solution)/shard_map/ppermute | solution.py:284
  99.0 44.9 %collective-permute-start.15 = (bf16[256,1024]{1,0:T(8,128)(2,1)}, bf16[256,1024]{1,0:T(8,128)(2,1)}, u32[]{:S(2)}, u32[]{:S(2)}) collective-permute-start(bf16[256,1024]{1,0:T(8,128)(2,1)} %get-tuple-element.38), channel_id=1, source_target_pairs={{0,4},{2,6},{4,0},{6,2},{8,12},{10,14},{12,8},{14,10},{16,20},{18,... | collective-permute-start | bytes 1572872 | tf_op jit(solution)/shard_map/ppermute | solution.py:284
  100.8 39.3 %collective-permute-start.18 = (bf16[512,1024]{1,0:T(8,128)(2,1)}, bf16[512,1024]{1,0:T(8,128)(2,1)}, u32[]{:S(2)}, u32[]{:S(2)}) collective-permute-start(bf16[512,1024]{1,0:T(8,128)(2,1)} %collective-permute-done.17.refs_3_.refs_8_), channel_id=1, source_target_pairs={{0,4},{2,6},{4,0},{6,2},{8,12},{10,14},{12,8},{14,10},{16,20},{18,... | collective-permute-start | bytes 3145736 | tf_op jit(solution)/shard_map/ppermute | solution.py:284
  108.0 99.3 %collective-permute-start.38 = (bf16[2048,512]{1,0:T(8,128)(2,1)}, bf16[2048,512]{1,0:T(8,128)(2,1)}, u32[]{:S(2)}, u32[]{:S(2)}) collective-permute-start(bf16[2048,512]{1,0:T(8,128)(2,1)} %get-tuple-element.35), channel_id=1, source_target_pairs={{0,1},{1,0},{2,3},{3,2},{4,5},{5,4},{6,7},{7,6},{8,9},{9,8},{10,11... | collective-permute-start | bytes 6291464 | tf_op jit(solution)/shard_map/ppermute | solution.py:287
  111.7 39.8 %collective-permute-start.22 = (bf16[512,1024]{1,0:T(8,128)(2,1)}, bf16[512,1024]{1,0:T(8,128)(2,1)}, u32[]{:S(2)}, u32[]{:S(2)}) collective-permute-start(bf16[512,1024]{1,0:T(8,128)(2,1)} %collective-permute-done.17.refs_3_.refs_8_), channel_id=1, source_target_pairs={{0,8},{2,10},{4,12},{6,14},{8,0},{10,2},{12,4},{14,6},{16,24},{18,... | collective-permute-start | bytes 3145736 | tf_op jit(solution)/shard_map/ppermute | solution.py:284
  137.4 55.6 %collective-permute-start.25 = (bf16[512,1024]{1,0:T(8,128)(2,1)}, bf16[512,1024]{1,0:T(8,128)(2,1)S(1)}, u32[]{:S(2)}, u32[]{:S(2)}) collective-permute-start(bf16[512,1024]{1,0:T(8,128)(2,1)} %collective-permute-done.21.refs_0_.refs_7_), channel_id=1, source_target_pairs={{0,4},{2,6},{4,0},{6,2},{8,12},{10,14},{12,8},{14,10},{16,20},{18,... | collective-permute-start | bytes 3145736 | tf_op jit(solution)/shard_map/ppermute | solution.py:284
  143.9 49.2 %collective-permute-start.27 = (bf16[384,1024]{1,0:T(8,128)(2,1)}, bf16[384,1024]{1,0:T(8,128)(2,1)}, u32[]{:S(2)}, u32[]{:S(2)}) collective-permute-start(bf16[384,1024]{1,0:T(8,128)(2,1)} %slice.111), channel_id=1, source_target_pairs={{0,8},{2,10},{4,12},{6,14},{8,0},{10,2},{12,4},{14,6},{16,24},{18,... | collective-permute-start | bytes 2359304 | tf_op jit(solution)/shard_map/ppermute | solution.py:284
  148.8 26.2 %collective-permute-start.16 = (bf16[256,1024]{1,0:T(8,128)(2,1)}, bf16[256,1024]{1,0:T(8,128)(2,1)}, u32[]{:S(2)}, u32[]{:S(2)}) collective-permute-start(bf16[256,1024]{1,0:T(8,128)(2,1)} %get-tuple-element.37), channel_id=1, source_target_pairs={{0,4},{2,6},{4,0},{6,2},{8,12},{10,14},{12,8},{14,10},{16,20},{18,... | collective-permute-start | bytes 1572872 | tf_op jit(solution)/shard_map/ppermute | solution.py:284
  164.4 28.7 %collective-permute-start.26 = (bf16[128,1024]{1,0:T(8,128)(2,1)}, bf16[128,1024]{1,0:T(8,128)(2,1)S(1)}, u32[]{:S(2)}, u32[]{:S(2)}) collective-permute-start(bf16[128,1024]{1,0:T(8,128)(2,1)} %slice.110), channel_id=1, source_target_pairs={{0,4},{2,6},{4,0},{6,2},{8,12},{10,14},{12,8},{14,10},{16,20},{18,... | collective-permute-start | bytes 786440 | tf_op jit(solution)/shard_map/ppermute | solution.py:284
  181.0 48.9 %collective-permute-start.19 = (bf16[2,2,256,512]{3,2,1,0:T(8,128)(2,1)}, bf16[2,2,256,512]{3,2,1,0:T(8,128)(2,1)}, u32[]{:S(2)}, u32[]{:S(2)}) collective-permute-start(bf16[2,2,256,512]{3,2,1,0:T(8,128)(2,1)} %get-tuple-element.24), channel_id=1, source_target_pairs={{0,2},{2,0},{4,6},{6,4},{8,10},{10,8},{12,14},{14,12},{16,18},{18,... | collective-permute-start | bytes 3145736 | tf_op jit(solution)/shard_map/ppermute | solution.py:284
  207.3 61.3 %collective-permute-start.34 = (bf16[2048,512]{1,0:T(8,128)(2,1)S(1)}, bf16[2048,512]{1,0:T(8,128)(2,1)}, u32[]{:S(2)}, u32[]{:S(2)}) collective-permute-start(bf16[2048,512]{1,0:T(8,128)(2,1)S(1)} %get-tuple-element.36.w_ref), channel_id=1, source_target_pairs={{0,2},{2,0},{4,6},{6,4},{8,10},{10,8},{12,14},{14,12},{16,18},{18,... | collective-permute-start | bytes 6291464 | tf_op jit(solution)/shard_map/ppermute | solution.py:284
  207.3 67.0 %collective-permute-start.39 = (bf16[2048,512]{1,0:T(8,128)(2,1)}, bf16[2048,512]{1,0:T(8,128)(2,1)}, u32[]{:S(2)}, u32[]{:S(2)}) collective-permute-start(bf16[2048,512]{1,0:T(8,128)(2,1)} %collective-permute-done.38), channel_id=1, source_target_pairs={{0,2},{2,0},{4,6},{6,4},{8,10},{10,8},{12,14},{14,12},{16,18},{18,... | collective-permute-start | bytes 6291464 | tf_op jit(solution)/shard_map/ppermute | solution.py:284
  228.7 39.8 %collective-permute-start.33 = (bf16[256,512]{1,0:T(8,128)(2,1)}, bf16[256,512]{1,0:T(8,128)(2,1)}, u32[]{:S(2)}, u32[]{:S(2)}) collective-permute-start(bf16[256,512]{1,0:T(8,128)(2,1)} %get-tuple-element.34), channel_id=1, source_target_pairs={{0,2},{2,0},{4,6},{6,4},{8,10},{10,8},{12,14},{14,12},{16,18},{18,... | collective-permute-start | bytes 786440 | tf_op jit(solution)/shard_map/ppermute | solution.py:284
  234.0 31.7 %collective-permute-start.20 = (bf16[2,256,512]{2,1,0:T(8,128)(2,1)S(1)}, bf16[2,256,512]{2,1,0:T(8,128)(2,1)S(1)}, u32[]{:S(2)}, u32[]{:S(2)}) collective-permute-start(bf16[2,256,512]{2,1,0:T(8,128)(2,1)S(1)} %fusion), channel_id=1, source_target_pairs={{0,1},{1,0},{2,3},{3,2},{4,5},{5,4},{6,7},{7,6},{8,9},{9,8},{10,11... | collective-permute-start | bytes 1572872 | tf_op jit(solution)/shard_map/ppermute | solution.py:287
  (39 other events, 630.7 us)

commit v3 on v2

--- a/solution.py
+++ b/solution.py
@@ -13,6 +13,12 @@
 FACTOR = HEAD_DIM ** (-0.5)
 F32 = jnp.float32
 BF16 = jnp.bfloat16
+
+
+def kernel_call(body, **kwargs):
+    return pl.pallas_call(
+        body, compiler_params=pltpu.CompilerParams(vmem_limit_bytes=20 * 2**20), **kwargs
+    )
 
 
 def dot_nt(a, b):
@@ -205,7 +211,7 @@
             pl.BlockSpec((2, 1, HEAD_DIM, HEAD_DIM), lambda j, b: (0, j, 0, 0)),
             pl.BlockSpec((1, HEAD_DIM, HEAD_DIM), lambda j, b: (j, 0, 0)),
         ]
-    out = pl.pallas_call(
+    out = kernel_call(
         body,
         out_shape=out_shape,
         grid_spec=pltpu.PrefetchScalarGridSpec(
@@ -249,7 +255,7 @@
             in_specs += [pl.BlockSpec(w.shape, lambda j, b: (0, 0)) for w in piece]
     out = pl.BlockSpec((2, n, tokens, half), lambda j, b: (0, 0, 0, j))
     shape = (2, n, tokens, rows)
-    return pl.pallas_call(
+    return kernel_call(
         body,
         out_shape=(jax.ShapeDtypeStruct(shape, F32), jax.ShapeDtypeStruct(shape, BF16)),
         grid_spec=pltpu.PrefetchScalarGridSpec(
@@ -262,10 +268,36 @@
     return total + mm(g, w, NT) + mm(g_other, w_other, NT)
 
 
-def home_kernel(sum_ref, g_ref, g_other_ref, w_ref, w_other_ref, out_ref):
-    out_ref[0] = add_two(
-        sum_ref[0], g_ref[...], g_other_ref[...], w_ref[...], w_other_ref[...]
-    )
+def home_kernel(g_ref, g_other_ref, w_ref, w_other_ref, *refs):
+    out_ref, triples = refs[-1], [refs[i : i + 3] for i in range(0, len(refs) - 1, 3)]
+    slot = pl.program_id(0)
+    total = None
+    for n, (keep, core, far) in enumerate(triples):
+        part = keep[0, 0] + core[0, 0].astype(F32) + far[0].astype(F32)
+        total = part if total is None else jnp.where(slot > n, part, total)
+    out_ref[0] = add_two(total, g_ref[...], g_other_ref[...], w_ref[...], w_other_ref[...])
+
+
+def fetch_kernel(*refs):
+    n = (len(refs) - 1) // 2
+    sems = refs[-1]
+    copies = [pltpu.make_async_copy(refs[i], refs[n + i], sems.at[i]) for i in range(n)]
+    for copy in copies:
+        copy.start()
+    for copy in copies:
+        copy.wait()
+
+
+def fetch(*arrays):
+    hbm = pl.BlockSpec(memory_space=pl.ANY)
+    vmem = pl.BlockSpec(memory_space=pltpu.VMEM)
+    return kernel_call(
+        fetch_kernel,
+        out_shape=[pltpu.VMEM(a.shape, a.dtype) for a in arrays],
+        in_specs=[hbm] * len(arrays),
+        out_specs=[vmem] * len(arrays),
+        scratch_shapes=[pltpu.SemaphoreType.DMA((len(arrays),))],
+    )(*arrays)
 
 
 def finish_kernel(base_ref, sum_ref, g_ref, g_other_ref, w_ref, w_other_ref, out_ref):
@@ -374,7 +406,7 @@
                 total = total + got.astype(F32)
 
         totals = jax.ShapeDtypeStruct(states.shape[1:], BF16)
-        state, total = pl.pallas_call(state_kernel, out_shape=(states, totals))(kv)
+        state, total = kernel_call(state_kernel, out_shape=(states, totals))(kv)
         outside, got, counts = scan(total, True)
         outside = outside + jnp.where(counts, got.astype(F32), 0.0)
         prefix = jnp.stack(
@@ -384,7 +416,7 @@
             ]
         ).astype(BF16)
         q_spec = pl.BlockSpec((tokens, n_cols), lambda n, g: (n, g))
-        gq = pl.pallas_call(
+        gq = kernel_call(
             grad_query_kernel,
             out_shape=jax.ShapeDtypeStruct((2 * tokens, groups * n_cols), BF16),
             grid=(2, groups),
@@ -405,7 +437,7 @@
             if after is not None:
                 keep = gate(keep, after)
             away = (keep[1] + got[1].astype(F32)).astype(BF16)
-            return keep[0], got[0], swap_y(away), away
+            return keep, got, swap_y(away), away
 
         sums = [back((0, 1))]
         sums.append(back((2,), sums[0][3]))
@@ -415,7 +447,7 @@
         inner = []
         for g in range(groups):
             inner.append(
-                pl.pallas_call(
+                kernel_call(
                     inner_kernel,
                     out_shape=jax.ShapeDtypeStruct((2 * tokens, 2 * HEAD_DIM), F32),
                     grid=(2,),
@@ -432,7 +464,7 @@
         flags = jnp.stack([counts, core == 0]).astype(jnp.int32)
         part = jax.ShapeDtypeStruct((tokens, 2 * groups * HEAD_DIM), BF16)
         vmem = pl.BlockSpec(memory_space=pltpu.VMEM)
-        gkv, gkv_other = pl.pallas_call(
+        gkv, gkv_other = kernel_call(
             outer_kernel,
             out_shape=(part, part),
             in_specs=[pl.BlockSpec(memory_space=pltpu.SMEM)] + [vmem] * (4 + groups),
@@ -440,32 +472,37 @@
         )(flags, kv, outside, got, gs, *inner)
         far_other, far = swap_y(gkv_other), swap_y(gkv)
         gkv_c, far_c = swap(gkv_other, C1), swap(far_other, C1)
-        home = jnp.concatenate(
-            [p[0] + p[1].astype(F32) + p[2].astype(F32) for p in sums], 0
-        )
-        slots, width = home.shape[0], home.shape[2]
-        home = pl.pallas_call(
+        slots, width = n_half, sums[0][0].shape[3]
+        block, steps = (1, tokens, width), []
+        for keep, core_got, far_got, _ in sums:
+            last = keep.shape[1] - 1
+            for array in (keep, core_got):
+                steps.append(
+                    (array, (1,) + block, lambda i, last=last: (0, jnp.minimum(i, last), 0, 0))
+                )
+            steps.append((far_got, block, lambda i, last=last: (jnp.minimum(i, last), 0, 0)))
+        home = kernel_call(
             home_kernel,
-            out_shape=jax.ShapeDtypeStruct(home.shape, F32),
+            out_shape=jax.ShapeDtypeStruct((slots, tokens, width), F32),
             grid=(slots,),
-            in_specs=[pl.BlockSpec((1, tokens, width), lambda i: (i, 0, 0))]
-            + [pl.BlockSpec(gkv.shape, lambda i: (0, 0))] * 2
-            + [pl.BlockSpec((width, w_home.shape[1]), lambda i: (i, 0))] * 2,
-            out_specs=pl.BlockSpec((1, tokens, width), lambda i: (i, 0, 0)),
-        )(home, gkv, gkv_c, w_home, w_home_c)
+            in_specs=[pl.BlockSpec(gkv.shape, lambda i: (0, 0))] * 2
+            + [pl.BlockSpec((width, w_home.shape[1]), lambda i: (i, 0))] * 2
+            + [pl.BlockSpec(shape, index) for _, shape, index in steps],
+            out_specs=pl.BlockSpec(block, lambda i: (i, 0, 0)),
+        )(gkv, gkv_c, w_home, w_home_c, *(array for array, _, _ in steps))
         by_slot = (slots, width, w_home.shape[1])
-        return pl.pallas_call(
-            finish_kernel,
-            out_shape=jax.ShapeDtypeStruct((tokens, slots * width), BF16),
-            in_specs=[pl.BlockSpec(memory_space=pltpu.SMEM)] + [vmem] * 5,
-            out_specs=vmem,
+        w_far = fetch(w_home_y.reshape(by_slot), w_home_cy.reshape(by_slot))
+        return kernel_call(
+    finish_kernel,
+    out_shape=jax.ShapeDtypeStruct((tokens, slots * width), BF16),
+    in_specs=[pl.BlockSpec(memory_space=pltpu.SMEM)] + [vmem] * 5,
+    out_specs=vmem,
         )(
             scalar(chip % per_half),
             home,
             far,
             far_c,
-            w_home_y.reshape(by_slot),
-            w_home_cy.reshape(by_slot),
+            *w_far,
         )
 
     return local

time: 281 us -> 287 us (1.021)
  waiting for transfers between devices: 121 us -> 163 us
  Pallas kernels: 67.8 us -> 43.5 us
  other arithmetic: 26 us -> 11.6 us
  local copies, waits for them, and re-layouts: 14.5 us -> 23.4 us
  starting transfers between devices: 50.9 us -> 43.3 us
    ppermute x33, waiting for transfers between devices: 80.6 us -> 138 us  [swap(): return lax.ppermute(value, 'seq', [(s, s ^ bit) for s in range(n_seq)])]
    pallas_call x15 -> x16, Pallas kernels: 67.8 us -> 43.5 us  [the longest x5 15.2 us: project_call(): kernel_call(body, out_shape=out_shape, grid_spec=pltpu.PrefetchScalarGrid...]
    ppermute x7, waiting for transfers between devices: 40.1 us -> 25.1 us  [swap_y(): return lax.ppermute(value, 'head', [(y, y ^ 1) for y in range(ys)])]
    unnamed x50 -> x90, local copies, waits for them, and re-layouts: 4.66 us -> 12.6 us
    select_n x1, other arithmetic: 6.65 us -> 2.58 us  [local(): w_home_y = swap_y(jnp.where(side == 0, high, low))]
    ppermute x7, starting transfers between devices: 13.4 us -> 9.46 us  [swap_y(): return lax.ppermute(value, 'head', [(y, y ^ 1) for y in range(ys)])]
    ppermute x33, starting transfers between devices: 37.5 us -> 33.9 us  [swap(): return lax.ppermute(value, 'seq', [(s, s ^ bit) for s in range(n_seq)])]
    add x3 -> x0, other arithmetic: 3.36 us -> none  [local(): p[0] + p[1].astype(F32) + p[2].astype(F32)]
  transfers between devices with their start and end apart: 40 -> 40, of which waited for: 14 -> 18; matrix products, arithmetic and copies ran while one was open for 14% -> 9% of each run, Pallas kernels for 22% -> 14%
where the time goes in v3:
time: 287 us; the launch traced here: 286 us
  waiting for transfers between devices  163 us (57%)
  Pallas kernels  43.5 us (15%)
  starting transfers between devices  43.3 us (15%)
  local copies, waits for them, and re-layouts  23.4 us (8%)
  other arithmetic  11.6 us (4%)
    ppermute x33, waiting for transfers between devices, swap(): return lax.ppermute(value, 'seq', [(s, s ^ bit) for s in range(n_seq)])  138 us
    ppermute x33, starting transfers between devices, swap(): return lax.ppermute(value, 'seq', [(s, s ^ bit) for s in range(n_seq)])  33.9 us
    ppermute x7, waiting for transfers between devices, swap_y(): return lax.ppermute(value, 'head', [(y, y ^ 1) for y in range(ys)])  25.1 us
    pallas_call x5, Pallas kernels, project_call(): kernel_call(body, out_shape=out_shape, grid_spec=pltpu.PrefetchScalarGrid...  15.2 us
    unnamed x90, local copies, waits for them, and re-layouts  12.6 us
    pallas_call x3, Pallas kernels, back_call(): kernel_call(body, out_shape=(jax.ShapeDtypeStruct(shape, F32), jax.ShapeD...  11.7 us
    ppermute x7, starting transfers between devices, swap_y(): return lax.ppermute(value, 'head', [(y, y ^ 1) for y in range(ys)])  9.46 us
  transfers between devices with their start and end apart: 40, of which 18 were waited for; matrix products, arithmetic and copies ran while one was open for 9% of the time, Pallas kernels for 14%

profile of v3, /device:TPU:0, one launch (start us, length us, event | category | flops | bytes accessed | tf_op | source)
XLA Modules:
  0.0 285.6 jit_solution(1910304887336295163)
XLA Ops:
  9.3 21.3 %collective-permute-done.6.refs_7_ = bf16[512,512]{1,0:T(8,128)(2,1)S(1)} collective-permute-done((bf16[512,512]{1,0:T(8,128)(2,1)S(1)}, bf16[512,512]{1,0:T(8,128)(2,1)S(1)}, u32[]{:S(2)}, u32[]{:S(2)}) %collective-permute-start.6) | collective-permute-done | bytes 524320 | tf_op jit(solution)/shard_map/ppermute | solution.py:316
  38.9 6.6 %collective-permute-done.8.refs_6_ = bf16[512,512]{1,0:T(8,128)(2,1)S(1)} collective-permute-done((bf16[512,512]{1,0:T(8,128)(2,1)S(1)}, bf16[512,512]{1,0:T(8,128)(2,1)S(1)}, u32[]{:S(2)}, u32[]{:S(2)}) %collective-permute-start.8) | collective-permute-done | bytes 524320 | tf_op jit(solution)/shard_map/ppermute | solution.py:316
  48.5 6.5 %collective-permute-done.4.refs_6_ = bf16[512,512]{1,0:T(8,128)(2,1)S(1)} collective-permute-done((bf16[512,512]{1,0:T(8,128)(2,1)S(1)}, bf16[512,512]{1,0:T(8,128)(2,1)S(1)}, u32[]{:S(2)}, u32[]{:S(2)}) %collective-permute-start.4) | collective-permute-done | bytes 524320 | tf_op jit(solution)/shard_map/ppermute | solution.py:316
  57.6 3.1 %collective-permute-start.14 = (bf16[512,1024]{1,0:T(8,128)(2,1)S(1)}, bf16[512,1024]{1,0:T(8,128)(2,1)}, u32[]{:S(2)}, u32[]{:S(2)}) collective-permute-start(bf16[512,1024]{1,0:T(8,128)(2,1)S(1)} %constant_dynamic-update-slice_fusion.6.refs_4_.refs_0_), channel_id=1, source_target_pairs={{0,16},{2,18},{4,20},{6,22},{8,24},{10,26},{12,28},{14,30},{16,0},... | collective-permute-start | bytes 3145736 | tf_op jit(solution)/shard_map/ppermute | solution.py:316
  64.6 10.0 %collective-permute-done.10.refs_5_ = bf16[512,512]{1,0:T(8,128)(2,1)S(1)} collective-permute-done((bf16[512,512]{1,0:T(8,128)(2,1)S(1)}, bf16[512,512]{1,0:T(8,128)(2,1)S(1)}, u32[]{:S(2)}, u32[]{:S(2)}) %collective-permute-start.10) | collective-permute-done | bytes 524320 | tf_op jit(solution)/shard_map/ppermute | solution.py:316
  75.3 10.1 %collective-permute-done.5.refs_4_ = bf16[512,512]{1,0:T(8,128)(2,1)S(1)} collective-permute-done((bf16[512,512]{1,0:T(8,128)(2,1)S(1)}, bf16[512,512]{1,0:T(8,128)(2,1)S(1)}, u32[]{:S(2)}, u32[]{:S(2)}) %collective-permute-start.5) | collective-permute-done | bytes 524320 | tf_op jit(solution)/shard_map/ppermute | solution.py:316
  89.4 16.6 %collective-permute-done.14.refs_8_.refs_3_ = bf16[512,1024]{1,0:T(8,128)(2,1)} collective-permute-done((bf16[512,1024]{1,0:T(8,128)(2,1)S(1)}, bf16[512,1024]{1,0:T(8,128)(2,1)}, u32[]{:S(2)}, u32[]{:S(2)}) %collective-permute-start.14) | collective-permute-done | bytes 1048608 | tf_op jit(solution)/shard_map/ppermute | solution.py:316
  110.1 10.4 %collective-permute-done.12.refs_7_.refs_0_ = bf16[512,1024]{1,0:T(8,128)(2,1)} collective-permute-done((bf16[512,1024]{1,0:T(8,128)(2,1)S(1)}, bf16[512,1024]{1,0:T(8,128)(2,1)}, u32[]{:S(2)}, u32[]{:S(2)}) %collective-permute-start.12) | collective-permute-done | bytes 1048608 | tf_op jit(solution)/shard_map/ppermute | solution.py:316
  129.6 13.9 %collective-permute-done.19.refs_5_.refs_1_ = bf16[256,1024]{1,0:T(8,128)(2,1)S(1)} collective-permute-done((bf16[256,1024]{1,0:T(8,128)(2,1)S(1)}, bf16[256,1024]{1,0:T(8,128)(2,1)S(1)}, u32[]{:S(2)}, u32[]{:S(2)}) %collective-permute-start.19) | collective-permute-done | bytes 524320 | tf_op jit(solution)/shard_map/ppermute | solution.py:316
  144.1 21.4 %collective-permute-done.26 = bf16[2,128,128]{2,1,0:T(8,128)(2,1)S(1)} collective-permute-done((bf16[2,128,128]{2,1,0:T(8,128)(2,1)S(1)}, bf16[2,128,128]{2,1,0:T(8,128)(2,1)S(1)}, u32[]{:S(2)}, u32[]{:S(2)}) %collective-permute-start.26) | collective-permute-done | bytes 65568 | tf_op jit(solution)/shard_map/ppermute | solution.py:316
  172.6 3.5 %collective-permute-start.28 = (bf16[2,128,128]{2,1,0:T(8,128)(2,1)}, bf16[2,128,128]{2,1,0:T(8,128)(2,1)}, u32[]{:S(2)}, u32[]{:S(2)}) collective-permute-start(bf16[2,128,128]{2,1,0:T(8,128)(2,1)} %fusion.7), channel_id=1, source_target_pairs={{0,16},{2,18},{4,20},{6,22},{8,24},{10,26},{12,28},{14,30},{16,0},... | collective-permute-start | bytes 196616 | tf_op jit(solution)/shard_map/ppermute | solution.py:316
  178.0 10.5 %collective-permute-done.28 = bf16[2,128,128]{2,1,0:T(8,128)(2,1)} collective-permute-done((bf16[2,128,128]{2,1,0:T(8,128)(2,1)}, bf16[2,128,128]{2,1,0:T(8,128)(2,1)}, u32[]{:S(2)}, u32[]{:S(2)}) %collective-permute-start.28) | collective-permute-done | bytes 65568 | tf_op jit(solution)/shard_map/ppermute | solution.py:316
  191.3 2.9 %shard_map.64.g_ref = bf16[512,1024]{1,0:T(8,128)(2,1)S(1)} custom-call(bf16[512,512]{1,0:T(8,128)(2,1)S(1)} %shard_map.56.k_ref.v_ref.kv_ref, bf16[512,512]{1,0:T(8,128)(2,1)S(1)} %shard_map.56.k_ref.v_ref.kv_ref, bf16[512,1024]{1,0:T(8,128)(2,1)S(1)} %pad_maximum_fusion.2.refs_6_.do_ref, bf16[2,2,128,128]{3,2,1,0:T(8,128)(2,1)S(1)} %pad_maximum_fusion.4.prefix_ref), custom_call_target="tpu_custom_call" | custom-call | tf_op jit(solution)/shard_map/pallas_call | solution.py:419
  194.3 5.0 %shard_map.65 = (f32[2,2,256,512]{3,2,1,0:T(8,128)S(1)}, bf16[2,2,256,512]{3,2,1,0:T(8,128)(2,1)}) custom-call(s32[1]{0:T(128)} %bitcast.4.side_ref, bf16[512,1024]{1,0:T(8,128)(2,1)S(1)} %shard_map.64.g_ref, bf16[512,1024]{1,0:T(8,128)(2,1)S(1)} %copy-done.3, bf16[256,1024]{1,0:T(8,128)(2,1)S(1)} %copy-done.29, ...), custom_call_target="tpu_custom_call" | custom-call | tf_op jit(solution)/shard_map/pallas_call | solution.py:258
  201.1 4.7 %shard_map.57.refs_4_ = f32[512,1024]{1,0:T(8,128)S(1)} custom-call(s32[1]{0:T(128)} %bitcast.3.base_ref, bf16[512,4096]{1,0:T(8,128)(2,1)S(1)} %copy-done.1, bf16[512,4096]{1,0:T(8,128)(2,1)S(1)} %copy-done.1, bf16[512,4096]{1,0:T(8,128)(2,1)S(1)} %copy-done.1, bf16[512,4096]{1,0:T(8,128)(2,1)S(1)} %copy-done.1, bf16[512,1024]{1,0:T(8,128)(2,1)S(1)} %copy-done.3, ...), custom_call_target="tpu_custom_call" | custom-call | tf_op jit(solution)/shard_map/pallas_call | solution.py:214
  208.4 3.5 %shard_map.59 = (bf16[512,1024]{1,0:T(8,128)(2,1)S(1)}, bf16[2,2,128,128]{3,2,1,0:T(8,128)(2,1)S(1)}, bf16[2,128,128]{2,1,0:T(8,128)(2,1)S(1)}) custom-call(s32[1]{0:T(128)} %bitcast.3.base_ref, bf16[512,4096]{1,0:T(8,128)(2,1)S(1)} %copy-done.1, bf16[512,4096]{1,0:T(8,128)(2,1)S(1)} %copy-done.1, bf16[512,1024]{1,0:T(8,128)(2,1)} %collective-permute-done.13.refs_2_.refs_0_, ...), custom_call_target="tpu_custom_call" | custom-call | tf_op jit(solution)/shard_map/pallas_call | solution.py:214
  213.0 4.1 %collective-permute-done.21 = bf16[2,128,128]{2,1,0:T(8,128)(2,1)S(1)} collective-permute-done((bf16[2,128,128]{2,1,0:T(8,128)(2,1)S(1)}, bf16[2,128,128]{2,1,0:T(8,128)(2,1)S(1)}, u32[]{:S(2)}, u32[]{:S(2)}) %collective-permute-start.21) | collective-permute-done | bytes 65568 | tf_op jit(solution)/shard_map/ppermute | solution.py:316
  217.8 4.2 %collective-permute-start.22 = (bf16[2,128,128]{2,1,0:T(8,128)(2,1)S(1)}, bf16[2,128,128]{2,1,0:T(8,128)(2,1)}, u32[]{:S(2)}, u32[]{:S(2)}) collective-permute-start(bf16[2,128,128]{2,1,0:T(8,128)(2,1)S(1)} %fusion.10), channel_id=1, source_target_pairs={{0,8},{2,10},{4,12},{6,14},{8,0},{10,2},{12,4},{14,6},{16,24},{18,... | collective-permute-start | bytes 196616 | tf_op jit(solution)/shard_map/ppermute | solution.py:316
  227.7 3.3 %shard_map.66 = (f32[2,1,256,512]{3,2,1,0:T(8,128)S(1)}, bf16[2,1,256,512]{3,2,1,0:T(8,128)(2,1)}) custom-call(s32[1]{0:T(128)} %bitcast.4.side_ref, bf16[512,1024]{1,0:T(8,128)(2,1)S(1)} %shard_map.64.g_ref, bf16[512,1024]{1,0:T(8,128)(2,1)} %collective-permute-done.12.refs_7_.refs_0_, bf16[512,1024]{1,0:T(8,128)(2,1)S(1)} %copy-done.9), custom_call_target="tpu_custom_call" | custom-call | tf_op jit(solution)/shard_map/pallas_call | solution.py:258
  232.1 3.4 %shard_map.67 = (f32[2,1,256,512]{3,2,1,0:T(8,128)S(1)}, bf16[2,1,256,512]{3,2,1,0:T(8,128)(2,1)}) custom-call(s32[1]{0:T(128)} %bitcast.4.side_ref, bf16[512,1024]{1,0:T(8,128)(2,1)S(1)} %shard_map.64.g_ref, bf16[512,1024]{1,0:T(8,128)(2,1)} %collective-permute-done.13.refs_2_.refs_0_, bf16[128,1024]{1,0:T(8,128)(2,1)S(1)} %copy-done.31, ...), custom_call_target="tpu_custom_call" | custom-call | tf_op jit(solution)/shard_map/pallas_call | solution.py:258
  249.8 4.7 %collective-permute-done.36 = bf16[256,512]{1,0:T(8,128)(2,1)S(1)} collective-permute-done((bf16[256,512]{1,0:T(8,128)(2,1)S(1)}, bf16[256,512]{1,0:T(8,128)(2,1)S(1)}, u32[]{:S(2)}, u32[]{:S(2)}) %collective-permute-start.36) | collective-permute-done | bytes 262176 | tf_op jit(solution)/shard_map/ppermute | solution.py:319
  256.5 14.8 %collective-permute-done.34.refs_8_ = bf16[1,256,512]{2,1,0:T(8,128)(2,1)S(1)} collective-permute-done((bf16[1,256,512]{2,1,0:T(8,128)(2,1)S(1)}, bf16[1,256,512]{2,1,0:T(8,128)(2,1)S(1)}, u32[]{:S(2)}, u32[]{:S(2)}) %collective-permute-start.34) | collective-permute-done | bytes 262176 | tf_op jit(solution)/shard_map/ppermute | solution.py:319
  271.4 5.6 %collective-permute-done.32.refs_5_ = bf16[1,256,512]{2,1,0:T(8,128)(2,1)S(1)} collective-permute-done((bf16[1,256,512]{2,1,0:T(8,128)(2,1)S(1)}, bf16[1,256,512]{2,1,0:T(8,128)(2,1)S(1)}, u32[]{:S(2)}, u32[]{:S(2)}) %collective-permute-start.32) | collective-permute-done | bytes 262176 | tf_op jit(solution)/shard_map/ppermute | solution.py:319
  277.0 4.1 %shard_map.68.sum_ref = f32[4,256,512]{2,1,0:T(8,128)S(1)} custom-call(bf16[256,512]{1,0:T(8,128)(2,1)S(1)} %get-tuple-element.26.g_ref, bf16[256,512]{1,0:T(8,128)(2,1)S(1)} %collective-permute-done.24.g_other_ref, bf16[2048,512]{1,0:T(8,128)(2,1)S(1)} %copy-done.4, bf16[2048,512]{1,0:T(8,128)(2,1)} %collective-permute-done.25.w_other_ref, ...), custom_call_target="tpu_custom_call" | custom-call | tf_op jit(solution)/shard_map/pallas_call | solution.py:484
  (189 shorter events, 90.7 us)
Async XLA Ops:
  1.7 33.3 %collective-permute-start = (bf16[256,2048]{1,0:T(8,128)(2,1)}, bf16[256,2048]{1,0:T(8,128)(2,1)}, u32[]{:S(2)}, u32[]{:S(2)}) collective-permute-start(bf16[256,2048]{1,0:T(8,128)(2,1)} %param.5), channel_id=1, source_target_pairs={{0,1},{1,0},{2,3},{3,2},{4,5},{5,4},{6,7},{7,6},{8,9},{9,8},{10,11... | collective-permute-start | bytes 3145736 | tf_op jit(solution)/shard_map/ppermute | solution.py:319
  4.4 26.2 %collective-permute-start.6 = (bf16[512,512]{1,0:T(8,128)(2,1)S(1)}, bf16[512,512]{1,0:T(8,128)(2,1)S(1)}, u32[]{:S(2)}, u32[]{:S(2)}) collective-permute-start(bf16[512,512]{1,0:T(8,128)(2,1)S(1)} %constant_dynamic-update-slice_fusion.7.refs_4_), channel_id=1, source_target_pairs={{0,16},{2,18},{4,20},{6,22},{8,24},{10,26},{12,28},{14,30},{16,0},... | collective-permute-start | bytes 1572872 | tf_op jit(solution)/shard_map/ppermute | solution.py:316
  9.3 38.7 %collective-permute-start.11 = (bf16[256,1024]{1,0:T(8,128)(2,1)}, bf16[256,1024]{1,0:T(8,128)(2,1)}, u32[]{:S(2)}, u32[]{:S(2)}) collective-permute-start(bf16[256,1024]{1,0:T(8,128)(2,1)} %get-tuple-element.43), channel_id=1, source_target_pairs={{0,2},{2,0},{4,6},{6,4},{8,10},{10,8},{12,14},{14,12},{16,18},{18,... | collective-permute-start | bytes 1572872 | tf_op jit(solution)/shard_map/ppermute | solution.py:316
  33.7 21.3 %collective-permute-start.4 = (bf16[512,512]{1,0:T(8,128)(2,1)S(1)}, bf16[512,512]{1,0:T(8,128)(2,1)S(1)}, u32[]{:S(2)}, u32[]{:S(2)}) collective-permute-start(bf16[512,512]{1,0:T(8,128)(2,1)S(1)} %constant_dynamic-update-slice_fusion.7.refs_4_), channel_id=1, source_target_pairs={{0,8},{2,10},{4,12},{6,14},{8,0},{10,2},{12,4},{14,6},{16,24},{18,... | collective-permute-start | bytes 1572872 | tf_op jit(solution)/shard_map/ppermute | solution.py:316
  37.4 83.1 %collective-permute-start.1 = (bf16[256,4096]{1,0:T(8,128)(2,1)}, bf16[256,4096]{1,0:T(8,128)(2,1)}, u32[]{:S(2)}, u32[]{:S(2)}) collective-permute-start(bf16[256,4096]{1,0:T(8,128)(2,1)} %constant_dynamic-update-slice_fusion), channel_id=1, source_target_pairs={{0,2},{2,0},{4,6},{6,4},{8,10},{10,8},{12,14},{14,12},{16,18},{18,... | collective-permute-start | bytes 6291464 | tf_op jit(solution)/shard_map/ppermute | solution.py:316
  48.0 26.7 %collective-permute-start.10 = (bf16[512,512]{1,0:T(8,128)(2,1)S(1)}, bf16[512,512]{1,0:T(8,128)(2,1)S(1)}, u32[]{:S(2)}, u32[]{:S(2)}) collective-permute-start(bf16[512,512]{1,0:T(8,128)(2,1)S(1)} %constant_dynamic-update-slice_fusion.7.refs_4_), channel_id=1, source_target_pairs={{0,4},{2,6},{4,0},{6,2},{8,12},{10,14},{12,8},{14,10},{16,20},{18,... | collective-permute-start | bytes 1572872 | tf_op jit(solution)/shard_map/ppermute | solution.py:316
  55.0 30.4 %collective-permute-start.5 = (bf16[512,512]{1,0:T(8,128)(2,1)S(1)}, bf16[512,512]{1,0:T(8,128)(2,1)S(1)}, u32[]{:S(2)}, u32[]{:S(2)}) collective-permute-start(bf16[512,512]{1,0:T(8,128)(2,1)S(1)} %collective-permute-done.4.refs_6_), channel_id=1, source_target_pairs={{0,4},{2,6},{4,0},{6,2},{8,12},{10,14},{12,8},{14,10},{16,20},{18,... | collective-permute-start | bytes 1572872 | tf_op jit(solution)/shard_map/ppermute | solution.py:316
  57.6 48.4 %collective-permute-start.14 = (bf16[512,1024]{1,0:T(8,128)(2,1)S(1)}, bf16[512,1024]{1,0:T(8,128)(2,1)}, u32[]{:S(2)}, u32[]{:S(2)}) collective-permute-start(bf16[512,1024]{1,0:T(8,128)(2,1)S(1)} %constant_dynamic-update-slice_fusion.6.refs_4_.refs_0_), channel_id=1, source_target_pairs={{0,16},{2,18},{4,20},{6,22},{8,24},{10,26},{12,28},{14,30},{16,0},... | collective-permute-start | bytes 3145736 | tf_op jit(solution)/shard_map/ppermute | solution.py:316
  63.5 43.9 %collective-permute-start.2 = (bf16[256,1024]{1,0:T(8,128)(2,1)}, bf16[256,1024]{1,0:T(8,128)(2,1)S(1)}, u32[]{:S(2)}, u32[]{:S(2)}) collective-permute-start(bf16[256,1024]{1,0:T(8,128)(2,1)} %get-tuple-element.46), channel_id=1, source_target_pairs={{0,2},{2,0},{4,6},{6,4},{8,10},{10,8},{12,14},{14,12},{16,18},{18,... | collective-permute-start | bytes 1572872 | tf_op jit(solution)/shard_map/ppermute | solution.py:316
  74.6 45.8 %collective-permute-start.12 = (bf16[512,1024]{1,0:T(8,128)(2,1)S(1)}, bf16[512,1024]{1,0:T(8,128)(2,1)}, u32[]{:S(2)}, u32[]{:S(2)}) collective-permute-start(bf16[512,1024]{1,0:T(8,128)(2,1)S(1)} %constant_dynamic-update-slice_fusion.6.refs_4_.refs_0_), channel_id=1, source_target_pairs={{0,8},{2,10},{4,12},{6,14},{8,0},{10,2},{12,4},{14,6},{16,24},{18,... | collective-permute-start | bytes 3145736 | tf_op jit(solution)/shard_map/ppermute | solution.py:316
  88.0 112.6 %collective-permute-start.38 = (bf16[2048,512]{1,0:T(8,128)(2,1)}, bf16[2048,512]{1,0:T(8,128)(2,1)}, u32[]{:S(2)}, u32[]{:S(2)}) collective-permute-start(bf16[2048,512]{1,0:T(8,128)(2,1)} %get-tuple-element.39), channel_id=1, source_target_pairs={{0,1},{1,0},{2,3},{3,2},{4,5},{5,4},{6,7},{7,6},{8,9},{9,8},{10,11... | collective-permute-start | bytes 6291464 | tf_op jit(solution)/shard_map/ppermute | solution.py:319
  106.0 60.0 %collective-permute-start.17 = (bf16[512,1024]{1,0:T(8,128)(2,1)}, bf16[512,1024]{1,0:T(8,128)(2,1)S(1)}, u32[]{:S(2)}, u32[]{:S(2)}) collective-permute-start(bf16[512,1024]{1,0:T(8,128)(2,1)} %collective-permute-done.14.refs_8_.refs_3_), channel_id=1, source_target_pairs={{0,4},{2,6},{4,0},{6,2},{8,12},{10,14},{12,8},{14,10},{16,20},{18,... | collective-permute-start | bytes 3145736 | tf_op jit(solution)/shard_map/ppermute | solution.py:316
  107.5 36.1 %collective-permute-start.19 = (bf16[256,1024]{1,0:T(8,128)(2,1)S(1)}, bf16[256,1024]{1,0:T(8,128)(2,1)S(1)}, u32[]{:S(2)}, u32[]{:S(2)}) collective-permute-start(bf16[256,1024]{1,0:T(8,128)(2,1)S(1)} %get-tuple-element.42), channel_id=1, source_target_pairs={{0,4},{2,6},{4,0},{6,2},{8,12},{10,14},{12,8},{14,10},{16,20},{18,... | collective-permute-start | bytes 1572872 | tf_op jit(solution)/shard_map/ppermute | solution.py:316
  120.5 52.1 %collective-permute-start.15 = (bf16[512,1024]{1,0:T(8,128)(2,1)}, bf16[512,1024]{1,0:T(8,128)(2,1)S(1)}, u32[]{:S(2)}, u32[]{:S(2)}) collective-permute-start(bf16[512,1024]{1,0:T(8,128)(2,1)} %collective-permute-done.14.refs_8_.refs_3_), channel_id=1, source_target_pairs={{0,8},{2,10},{4,12},{6,14},{8,0},{10,2},{12,4},{14,6},{16,24},{18,... | collective-permute-start | bytes 3145736 | tf_op jit(solution)/shard_map/ppermute | solution.py:316
  120.5 80.1 %collective-permute-start.13 = (bf16[512,1024]{1,0:T(8,128)(2,1)}, bf16[512,1024]{1,0:T(8,128)(2,1)}, u32[]{:S(2)}, u32[]{:S(2)}) collective-permute-start(bf16[512,1024]{1,0:T(8,128)(2,1)} %collective-permute-done.12.refs_7_.refs_0_), channel_id=1, source_target_pairs={{0,4},{2,6},{4,0},{6,2},{8,12},{10,14},{12,8},{14,10},{16,20},{18,... | collective-permute-start | bytes 3145736 | tf_op jit(solution)/shard_map/ppermute | solution.py:316
  143.5 22.0 %collective-permute-start.26 = (bf16[2,128,128]{2,1,0:T(8,128)(2,1)S(1)}, bf16[2,128,128]{2,1,0:T(8,128)(2,1)S(1)}, u32[]{:S(2)}, u32[]{:S(2)}) collective-permute-start(bf16[2,128,128]{2,1,0:T(8,128)(2,1)S(1)} %get-tuple-element.28), channel_id=1, source_target_pairs={{0,4},{2,6},{4,0},{6,2},{8,12},{10,14},{12,8},{14,10},{16,20},{18,... | collective-permute-start | bytes 196616 | tf_op jit(solution)/shard_map/ppermute | solution.py:316
  170.4 38.0 %collective-permute-start.18 = (bf16[384,1024]{1,0:T(8,128)(2,1)}, bf16[384,1024]{1,0:T(8,128)(2,1)S(1)}, u32[]{:S(2)}, u32[]{:S(2)}) collective-permute-start(bf16[384,1024]{1,0:T(8,128)(2,1)} %slice.81), channel_id=1, source_target_pairs={{0,8},{2,10},{4,12},{6,14},{8,0},{10,2},{12,4},{14,6},{16,24},{18,... | collective-permute-start | bytes 2359304 | tf_op jit(solution)/shard_map/ppermute | solution.py:316
  177.9 77.9 %collective-permute-start.25 = (bf16[2048,512]{1,0:T(8,128)(2,1)}, bf16[2048,512]{1,0:T(8,128)(2,1)}, u32[]{:S(2)}, u32[]{:S(2)}) collective-permute-start(bf16[2048,512]{1,0:T(8,128)(2,1)} %get-tuple-element.40.w_ref), channel_id=1, source_target_pairs={{0,2},{2,0},{4,6},{6,4},{8,10},{10,8},{12,14},{14,12},{16,18},{18,... | collective-permute-start | bytes 6291464 | tf_op jit(solution)/shard_map/ppermute | solution.py:316
  200.6 43.2 %collective-permute-start.29 = (bf16[2,2,256,512]{3,2,1,0:T(8,128)(2,1)}, bf16[2,2,256,512]{3,2,1,0:T(8,128)(2,1)}, u32[]{:S(2)}, u32[]{:S(2)}) collective-permute-start(bf16[2,2,256,512]{3,2,1,0:T(8,128)(2,1)} %get-tuple-element.31), channel_id=1, source_target_pairs={{0,2},{2,0},{4,6},{6,4},{8,10},{10,8},{12,14},{14,12},{16,18},{18,... | collective-permute-start | bytes 3145736 | tf_op jit(solution)/shard_map/ppermute | solution.py:316
  200.6 80.5 %collective-permute-start.39 = (bf16[2048,512]{1,0:T(8,128)(2,1)}, bf16[2048,512]{1,0:T(8,128)(2,1)}, u32[]{:S(2)}, u32[]{:S(2)}) collective-permute-start(bf16[2048,512]{1,0:T(8,128)(2,1)} %collective-permute-done.38), channel_id=1, source_target_pairs={{0,2},{2,0},{4,6},{6,4},{8,10},{10,8},{12,14},{14,12},{16,18},{18,... | collective-permute-start | bytes 6291464 | tf_op jit(solution)/shard_map/ppermute | solution.py:316
  246.6 30.3 %collective-permute-start.30 = (bf16[2,256,512]{2,1,0:T(8,128)(2,1)S(1)}, bf16[2,256,512]{2,1,0:T(8,128)(2,1)S(1)}, u32[]{:S(2)}, u32[]{:S(2)}) collective-permute-start(bf16[2,256,512]{2,1,0:T(8,128)(2,1)S(1)} %fusion), channel_id=1, source_target_pairs={{0,1},{1,0},{2,3},{3,2},{4,5},{5,4},{6,7},{7,6},{8,9},{9,8},{10,11... | collective-permute-start | bytes 1572872 | tf_op jit(solution)/shard_map/ppermute | solution.py:319
  247.4 23.9 %collective-permute-start.34 = (bf16[1,256,512]{2,1,0:T(8,128)(2,1)S(1)}, bf16[1,256,512]{2,1,0:T(8,128)(2,1)S(1)}, u32[]{:S(2)}, u32[]{:S(2)}) collective-permute-start(bf16[1,256,512]{2,1,0:T(8,128)(2,1)S(1)} %fusion.2), channel_id=1, source_target_pairs={{0,1},{1,0},{2,3},{3,2},{4,5},{5,4},{6,7},{7,6},{8,9},{9,8},{10,11... | collective-permute-start | bytes 786440 | tf_op jit(solution)/shard_map/ppermute | solution.py:319
  254.5 22.5 %collective-permute-start.32 = (bf16[1,256,512]{2,1,0:T(8,128)(2,1)S(1)}, bf16[1,256,512]{2,1,0:T(8,128)(2,1)S(1)}, u32[]{:S(2)}, u32[]{:S(2)}) collective-permute-start(bf16[1,256,512]{2,1,0:T(8,128)(2,1)S(1)} %fusion.1), channel_id=1, source_target_pairs={{0,1},{1,0},{2,3},{3,2},{4,5},{5,4},{6,7},{7,6},{8,9},{9,8},{10,11... | collective-permute-start | bytes 786440 | tf_op jit(solution)/shard_map/ppermute | solution.py:319
  255.8 27.6 %collective-permute-start.35 = (bf16[256,512]{1,0:T(8,128)(2,1)S(1)}, bf16[256,512]{1,0:T(8,128)(2,1)S(1)}, u32[]{:S(2)}, u32[]{:S(2)}) collective-permute-start(bf16[256,512]{1,0:T(8,128)(2,1)S(1)} %get-tuple-element.26.g_ref), channel_id=1, source_target_pairs={{0,1},{1,0},{2,3},{3,2},{4,5},{5,4},{6,7},{7,6},{8,9},{9,8},{10,11... | collective-permute-start | bytes 786440 | tf_op jit(solution)/shard_map/ppermute | solution.py:319
  (59 other events, 632.5 us)

commit v4 on v3

--- a/solution.py
+++ b/solution.py
@@ -387,18 +387,29 @@
         n_half = chips // ys
         low, high = jnp.concatenate(w_kv[:n_half], 0), jnp.concatenate(w_kv[n_half:], 0)
         w_home = jnp.where(side == 0, low, high)
-        w_home_y = swap_y(jnp.where(side == 0, high, low))
+
+        def away_rows(first):
+            here = jnp.concatenate(w_kv[first:n_half:2], 0)
+            there = jnp.concatenate(w_kv[n_half + first :: 2], 0)
+            got = swap_y(jnp.where(side == 0, there, here))
+            return got.reshape(n_half // 2, 1, rows, got.shape[1])
+
+        rows = chunk_a.shape[0]
+        w_home_y = jnp.concatenate([away_rows(0), away_rows(1)], 1)
+        w_home_y = w_home_y.reshape(w_home.shape)
         w_home_c = swap(w_home, C1)
         w_home_cy = swap(w_home_y, C1)
 
         n_cols = GROUP * HEAD_DIM
         states = jax.ShapeDtypeStruct((2, groups, HEAD_DIM, HEAD_DIM), BF16)
 
-        def scan(total, ahead):
+        def scan(total, ahead, after=None):
             total = total.astype(F32)
             outside = jnp.zeros_like(total)
             for bit, at in ((X1, x), (Z1, z % 2), (Z2, z // 2)):
                 got = swap(total.astype(BF16), bit)
+                if after is not None and bit == Z1:
+                    got = gate(got, after)
                 counts = (at == 1) == ahead
                 if bit == Z2:
                     return outside, got, counts
@@ -443,7 +454,8 @@
         sums.append(back((2,), sums[0][3]))
         q_sum = project(w_q, (5, 6), q_sum, F32)
         q, gs, total = project(w_q, (3, 7), q_sum, BF16, do_all)
-        outside, got, counts = scan(total, False)
+        sums.append(back((3,)))
+        outside, got, counts = scan(total, False, sums[2][3])
         inner = []
         for g in range(groups):
             inner.append(
@@ -460,7 +472,6 @@
                     out_specs=pl.BlockSpec((tokens, 2 * HEAD_DIM), lambda n: (n, 0)),
                 )(q, kv, kv, do_all)
             )
-        sums.append(back((3,)))
         flags = jnp.stack([counts, core == 0]).astype(jnp.int32)
         part = jax.ShapeDtypeStruct((tokens, 2 * groups * HEAD_DIM), BF16)
         vmem = pl.BlockSpec(memory_space=pltpu.VMEM)

time: 287 us -> 318 us (1.11)
  starting transfers between devices: 43.3 us -> 89.2 us
  local copies, waits for them, and re-layouts: 23.4 us -> 11.3 us
  waiting for transfers between devices: 163 us -> 159 us
    ppermute x33, starting transfers between devices: 33.9 us -> 77.3 us  [swap(): return lax.ppermute(value, 'seq', [(s, s ^ bit) for s in range(n_seq)])]
    ppermute x33, waiting for transfers between devices: 138 us -> 117 us  [swap(): return lax.ppermute(value, 'seq', [(s, s ^ bit) for s in range(n_seq)])]
    ppermute x7 -> x8, waiting for transfers between devices: 25.1 us -> 42.3 us  [swap_y(): return lax.ppermute(value, 'head', [(y, y ^ 1) for y in range(ys)])]
    unnamed x90 -> x33, local copies, waits for them, and re-layouts: 12.6 us -> 4.62 us
    select_n x1 -> x3, other arithmetic: 2.58 us -> 5.87 us  [the longest x2 3.07 us: away_rows(): got = swap_y(jnp.where(side == 0, there, here))]
    ppermute x7 -> x8, starting transfers between devices: 9.46 us -> 11.9 us  [swap_y(): return lax.ppermute(value, 'head', [(y, y ^ 1) for y in range(ys)])]
  transfers between devices with their start and end apart: 40 -> 41, of which waited for: 18 -> 12; matrix products, arithmetic and copies ran while one was open for 9% -> 7% of each run, Pallas kernels for 14% -> 13%
where the time goes in v4:
time: 318 us; the launch traced here: 317 us
  waiting for transfers between devices  159 us (50%)
  starting transfers between devices  89.2 us (28%)
  Pallas kernels  43.1 us (14%)
  other arithmetic  13.8 us (4%)
  local copies, waits for them, and re-layouts  11.3 us (4%)
    ppermute x33, waiting for transfers between devices, swap(): return lax.ppermute(value, 'seq', [(s, s ^ bit) for s in range(n_seq)])  117 us
    ppermute x33, starting transfers between devices, swap(): return lax.ppermute(value, 'seq', [(s, s ^ bit) for s in range(n_seq)])  77.3 us
    ppermute x8, waiting for transfers between devices, swap_y(): return lax.ppermute(value, 'head', [(y, y ^ 1) for y in range(ys)])  42.3 us
    pallas_call x5, Pallas kernels, project_call(): kernel_call(body, out_shape=out_shape, grid_spec=pltpu.PrefetchScalarGrid...  16.4 us
    ppermute x8, starting transfers between devices, swap_y(): return lax.ppermute(value, 'head', [(y, y ^ 1) for y in range(ys)])  11.9 us
    pallas_call x3, Pallas kernels, back_call(): kernel_call(body, out_shape=(jax.ShapeDtypeStruct(shape, F32), jax.ShapeD...  10 us
  transfers between devices with their start and end apart: 41, of which 12 were waited for; matrix products, arithmetic and copies ran while one was open for 7% of the time, Pallas kernels for 13%

profile of v4, /device:TPU:0, one launch (start us, length us, event | category | flops | bytes accessed | tf_op | source)
XLA Modules:
  0.0 316.9 jit_solution(14006054368818206906)
XLA Ops:
  0.0 3.0 collective-permute-start
  8.0 18.5 %collective-permute-done = bf16[256,2048]{1,0:T(8,128)(2,1)} collective-permute-done((bf16[256,2048]{1,0:T(8,128)(2,1)}, bf16[256,2048]{1,0:T(8,128)(2,1)}, u32[]{:S(2)}, u32[]{:S(2)}) %collective-permute-start) | collective-permute-done | bytes 1048608 | tf_op jit(solution)/shard_map/ppermute | solution.py:319
  37.7 18.7 %collective-permute-done.4.refs_6_ = bf16[512,512]{1,0:T(8,128)(2,1)S(1)} collective-permute-done((bf16[512,512]{1,0:T(8,128)(2,1)S(1)}, bf16[512,512]{1,0:T(8,128)(2,1)S(1)}, u32[]{:S(2)}, u32[]{:S(2)}) %collective-permute-start.4) | collective-permute-done | bytes 524320 | tf_op jit(solution)/shard_map/ppermute | solution.py:316
  58.0 24.6 %collective-permute-done.6.refs_7_ = bf16[512,512]{1,0:T(8,128)(2,1)} collective-permute-done((bf16[512,512]{1,0:T(8,128)(2,1)S(1)}, bf16[512,512]{1,0:T(8,128)(2,1)}, u32[]{:S(2)}, u32[]{:S(2)}) %collective-permute-start.6) | collective-permute-done | bytes 524320 | tf_op jit(solution)/shard_map/ppermute | solution.py:316
  86.2 43.8 %collective-permute-done.8.refs_6_ = bf16[512,512]{1,0:T(8,128)(2,1)} collective-permute-done((bf16[512,512]{1,0:T(8,128)(2,1)}, bf16[512,512]{1,0:T(8,128)(2,1)}, u32[]{:S(2)}, u32[]{:S(2)}) %collective-permute-start.8) | collective-permute-done | bytes 524320 | tf_op jit(solution)/shard_map/ppermute | solution.py:316
  137.2 8.4 %collective-permute-done.9.refs_7_ = bf16[512,512]{1,0:T(8,128)(2,1)} collective-permute-done((bf16[512,512]{1,0:T(8,128)(2,1)}, bf16[512,512]{1,0:T(8,128)(2,1)}, u32[]{:S(2)}, u32[]{:S(2)}) %collective-permute-start.9) | collective-permute-done | bytes 524320 | tf_op jit(solution)/shard_map/ppermute | solution.py:316
  150.7 2.7 pad_maximum_fusion.refs_0_.refs_1_.refs_2_.refs_3_
  153.4 2.7 shard_map.55.refs_8_
  162.4 7.5 %collective-permute-done.23 = bf16[2,128,128]{2,1,0:T(8,128)(2,1)S(1)} collective-permute-done((bf16[2,128,128]{2,1,0:T(8,128)(2,1)S(1)}, bf16[2,128,128]{2,1,0:T(8,128)(2,1)S(1)}, u32[]{:S(2)}, u32[]{:S(2)}) %collective-permute-start.23) | collective-permute-done | bytes 65568 | tf_op jit(solution)/shard_map/ppermute | solution.py:316
  172.5 2.8 maximum_select_fusion.w_ref
  175.3 7.7 %collective-permute-done.24 = bf16[2,128,128]{2,1,0:T(8,128)(2,1)S(1)} collective-permute-done((bf16[2,128,128]{2,1,0:T(8,128)(2,1)S(1)}, bf16[2,128,128]{2,1,0:T(8,128)(2,1)S(1)}, u32[]{:S(2)}, u32[]{:S(2)}) %collective-permute-start.24) | collective-permute-done | bytes 65568 | tf_op jit(solution)/shard_map/ppermute | solution.py:316
  185.2 36.3 %collective-permute-start.25 = (bf16[2,128,128]{2,1,0:T(8,128)(2,1)S(1)}, bf16[2,128,128]{2,1,0:T(8,128)(2,1)S(1)}, u32[]{:S(2)}, u32[]{:S(2)}) collective-permute-start(bf16[2,128,128]{2,1,0:T(8,128)(2,1)S(1)} %fusion.6), channel_id=1, source_target_pairs={{0,16},{2,18},{4,20},{6,22},{8,24},{10,26},{12,28},{14,30},{16,0},... | collective-permute-start | bytes 196616 | tf_op jit(solution)/shard_map/ppermute | solution.py:316
  225.3 2.9 shard_map.61.g_ref
  231.0 4.7 %shard_map.66 = (f32[2,2,256,512]{3,2,1,0:T(8,128)S(1)}, bf16[2,2,256,512]{3,2,1,0:T(8,128)(2,1)}) custom-call(s32[1]{0:T(128)} %bitcast.4.side_ref, bf16[512,1024]{1,0:T(8,128)(2,1)S(1)} %shard_map.61.g_ref, bf16[512,1024]{1,0:T(8,128)(2,1)S(1)} %copy-done.1, bf16[256,1024]{1,0:T(8,128)(2,1)S(1)} %collective-permute-done.19.refs_5_.refs_1_, ...), custom_call_target="tpu_custom_call" | custom-call | tf_op jit(solution)/shard_map/pallas_call | solution.py:258
  237.4 4.6 %shard_map.57.refs_4_ = f32[512,1024]{1,0:T(8,128)S(1)} custom-call(s32[1]{0:T(128)} %bitcast.3.base_ref, bf16[512,4096]{1,0:T(8,128)(2,1)S(1)} %pad_maximum_fusion.refs_0_.refs_1_.refs_2_.refs_3_, bf16[512,4096]{1,0:T(8,128)(2,1)S(1)} %pad_maximum_fusion.refs_0_.refs_1_.refs_2_.refs_3_, ...), custom_call_target="tpu_custom_call" | custom-call | tf_op jit(solution)/shard_map/pallas_call | solution.py:214
  242.1 3.6 %shard_map.58.refs_5_ = f32[512,1024]{1,0:T(8,128)S(1)} custom-call(s32[1]{0:T(128)} %bitcast.3.base_ref, bf16[512,4096]{1,0:T(8,128)(2,1)S(1)} %pad_maximum_fusion.refs_0_.refs_1_.refs_2_.refs_3_, bf16[512,4096]{1,0:T(8,128)(2,1)S(1)} %pad_maximum_fusion.refs_0_.refs_1_.refs_2_.refs_3_, bf16[512,1024]{1,0:T(8,128)(2,1)S(1)} %collective-permute-done.17.refs_2_.refs_4_, ...), custom_call_target="tpu_custom_call" | custom-call | tf_op jit(solution)/shard_map/pallas_call | solution.py:214
  245.6 2.8 shard_map.59
  250.9 3.0 shard_map.67
  254.9 3.7 %collective-permute-done.22 = bf16[2,128,128]{2,1,0:T(8,128)(2,1)S(1)} collective-permute-done((bf16[2,128,128]{2,1,0:T(8,128)(2,1)S(1)}, bf16[2,128,128]{2,1,0:T(8,128)(2,1)S(1)}, u32[]{:S(2)}, u32[]{:S(2)}) %collective-permute-start.22) | collective-permute-done | bytes 65568 | tf_op jit(solution)/shard_map/ppermute | solution.py:316
  258.6 13.7 %collective-permute-start.27 = (bf16[2,128,128]{2,1,0:T(8,128)(2,1)S(1)}, bf16[2,128,128]{2,1,0:T(8,128)(2,1)S(1)}, u32[]{:S(2)}, u32[]{:S(2)}) collective-permute-start(bf16[2,128,128]{2,1,0:T(8,128)(2,1)S(1)} %get-tuple-element.57), channel_id=1, source_target_pairs={{0,16},{2,18},{4,20},{6,22},{8,24},{10,26},{12,28},{14,30},{16,0},... | collective-permute-start | bytes 196616 | tf_op jit(solution)/shard_map/ppermute | solution.py:316
  282.2 3.3 %collective-permute-done.34.refs_8_ = bf16[1,256,512]{2,1,0:T(8,128)(2,1)S(1)} collective-permute-done((bf16[1,256,512]{2,1,0:T(8,128)(2,1)S(1)}, bf16[1,256,512]{2,1,0:T(8,128)(2,1)S(1)}, u32[]{:S(2)}, u32[]{:S(2)}) %collective-permute-start.34) | collective-permute-done | bytes 262176 | tf_op jit(solution)/shard_map/ppermute | solution.py:319
  287.5 14.8 %collective-permute-done.36 = bf16[256,512]{1,0:T(8,128)(2,1)S(1)} collective-permute-done((bf16[256,512]{1,0:T(8,128)(2,1)S(1)}, bf16[256,512]{1,0:T(8,128)(2,1)S(1)}, u32[]{:S(2)}, u32[]{:S(2)}) %collective-permute-start.36) | collective-permute-done | bytes 262176 | tf_op jit(solution)/shard_map/ppermute | solution.py:319
  302.4 5.6 %collective-permute-done.33.refs_5_ = bf16[1,256,512]{2,1,0:T(8,128)(2,1)S(1)} collective-permute-done((bf16[1,256,512]{2,1,0:T(8,128)(2,1)S(1)}, bf16[1,256,512]{2,1,0:T(8,128)(2,1)S(1)}, u32[]{:S(2)}, u32[]{:S(2)}) %collective-permute-start.33) | collective-permute-done | bytes 262176 | tf_op jit(solution)/shard_map/ppermute | solution.py:319
  308.0 4.4 %shard_map.68.sum_ref = f32[4,256,512]{2,1,0:T(8,128)S(1)} custom-call(bf16[256,512]{1,0:T(8,128)(2,1)S(1)} %get-tuple-element.32.g_ref, bf16[256,512]{1,0:T(8,128)(2,1)S(1)} %collective-permute-done.28.g_other_ref, bf16[2048,512]{1,0:T(8,128)(2,1)} %maximum_select_fusion.w_ref, bf16[2048,512]{1,0:T(8,128)(2,1)} %collective-permute-done.29.w_other_ref, ...), custom_call_target="tpu_custom_call" | custom-call | tf_op jit(solution)/shard_map/pallas_call | solution.py:495
  (136 shorter events, 72.4 us)
Async XLA Ops:
  5.1 30.7 %collective-permute-start.11 = (bf16[256,1024]{1,0:T(8,128)(2,1)S(1)}, bf16[256,1024]{1,0:T(8,128)(2,1)S(1)}, u32[]{:S(2)}, u32[]{:S(2)}) collective-permute-start(bf16[256,1024]{1,0:T(8,128)(2,1)S(1)} %get-tuple-element.43), channel_id=1, source_target_pairs={{0,2},{2,0},{4,6},{6,4},{8,10},{10,8},{12,14},{14,12},{16,18},{18,... | collective-permute-start | bytes 1572872 | tf_op jit(solution)/shard_map/ppermute | solution.py:316
  28.8 120.3 %collective-permute-start.1 = (bf16[256,4096]{1,0:T(8,128)(2,1)}, bf16[256,4096]{1,0:T(8,128)(2,1)}, u32[]{:S(2)}, u32[]{:S(2)}) collective-permute-start(bf16[256,4096]{1,0:T(8,128)(2,1)} %constant_dynamic-update-slice_fusion), channel_id=1, source_target_pairs={{0,2},{2,0},{4,6},{6,4},{8,10},{10,8},{12,14},{14,12},{16,18},{18,... | collective-permute-start | bytes 6291464 | tf_op jit(solution)/shard_map/ppermute | solution.py:316
  33.2 49.5 %collective-permute-start.6 = (bf16[512,512]{1,0:T(8,128)(2,1)S(1)}, bf16[512,512]{1,0:T(8,128)(2,1)}, u32[]{:S(2)}, u32[]{:S(2)}) collective-permute-start(bf16[512,512]{1,0:T(8,128)(2,1)S(1)} %constant_dynamic-update-slice_fusion.3.refs_4_), channel_id=1, source_target_pairs={{0,16},{2,18},{4,20},{6,22},{8,24},{10,26},{12,28},{14,30},{16,0},... | collective-permute-start | bytes 1572872 | tf_op jit(solution)/shard_map/ppermute | solution.py:316
  35.8 46.9 %collective-permute-start.10 = (bf16[512,512]{1,0:T(8,128)(2,1)S(1)}, bf16[512,512]{1,0:T(8,128)(2,1)S(1)}, u32[]{:S(2)}, u32[]{:S(2)}) collective-permute-start(bf16[512,512]{1,0:T(8,128)(2,1)S(1)} %constant_dynamic-update-slice_fusion.3.refs_4_), channel_id=1, source_target_pairs={{0,4},{2,6},{4,0},{6,2},{8,12},{10,14},{12,8},{14,10},{16,20},{18,... | collective-permute-start | bytes 1572872 | tf_op jit(solution)/shard_map/ppermute | solution.py:316
  37.3 95.2 %collective-permute-start.14 = (bf16[512,1024]{1,0:T(8,128)(2,1)S(1)}, bf16[512,1024]{1,0:T(8,128)(2,1)}, u32[]{:S(2)}, u32[]{:S(2)}) collective-permute-start(bf16[512,1024]{1,0:T(8,128)(2,1)S(1)} %constant_dynamic-update-slice_fusion.2.refs_4_.refs_0_), channel_id=1, source_target_pairs={{0,16},{2,18},{4,20},{6,22},{8,24},{10,26},{12,28},{14,30},{16,0},... | collective-permute-start | bytes 3145736 | tf_op jit(solution)/shard_map/ppermute | solution.py:316
  56.4 28.3 %collective-permute-start.5 = (bf16[512,512]{1,0:T(8,128)(2,1)S(1)}, bf16[512,512]{1,0:T(8,128)(2,1)S(1)}, u32[]{:S(2)}, u32[]{:S(2)}) collective-permute-start(bf16[512,512]{1,0:T(8,128)(2,1)S(1)} %collective-permute-done.4.refs_6_), channel_id=1, source_target_pairs={{0,4},{2,6},{4,0},{6,2},{8,12},{10,14},{12,8},{14,10},{16,20},{18,... | collective-permute-start | bytes 1572872 | tf_op jit(solution)/shard_map/ppermute | solution.py:316
  82.7 52.9 %collective-permute-start.12 = (bf16[512,1024]{1,0:T(8,128)(2,1)S(1)}, bf16[512,1024]{1,0:T(8,128)(2,1)}, u32[]{:S(2)}, u32[]{:S(2)}) collective-permute-start(bf16[512,1024]{1,0:T(8,128)(2,1)S(1)} %constant_dynamic-update-slice_fusion.2.refs_4_.refs_0_), channel_id=1, source_target_pairs={{0,8},{2,10},{4,12},{6,14},{8,0},{10,2},{12,4},{14,6},{16,24},{18,... | collective-permute-start | bytes 3145736 | tf_op jit(solution)/shard_map/ppermute | solution.py:316
  82.7 47.3 %collective-permute-start.8 = (bf16[512,512]{1,0:T(8,128)(2,1)}, bf16[512,512]{1,0:T(8,128)(2,1)}, u32[]{:S(2)}, u32[]{:S(2)}) collective-permute-start(bf16[512,512]{1,0:T(8,128)(2,1)} %collective-permute-done.6.refs_7_), channel_id=1, source_target_pairs={{0,8},{2,10},{4,12},{6,14},{8,0},{10,2},{12,4},{14,6},{16,24},{18,... | collective-permute-start | bytes 1572872 | tf_op jit(solution)/shard_map/ppermute | solution.py:316
  84.7 49.1 %collective-permute-start.7 = (bf16[512,512]{1,0:T(8,128)(2,1)}, bf16[512,512]{1,0:T(8,128)(2,1)}, u32[]{:S(2)}, u32[]{:S(2)}) collective-permute-start(bf16[512,512]{1,0:T(8,128)(2,1)} %collective-permute-done.6.refs_7_), channel_id=1, source_target_pairs={{0,4},{2,6},{4,0},{6,2},{8,12},{10,14},{12,8},{14,10},{16,20},{18,... | collective-permute-start | bytes 1572872 | tf_op jit(solution)/shard_map/ppermute | solution.py:316
  132.5 26.6 %collective-permute-start.15 = (bf16[512,1024]{1,0:T(8,128)(2,1)}, bf16[512,1024]{1,0:T(8,128)(2,1)}, u32[]{:S(2)}, u32[]{:S(2)}) collective-permute-start(bf16[512,1024]{1,0:T(8,128)(2,1)} %collective-permute-done.14.refs_8_.refs_3_), channel_id=1, source_target_pairs={{0,8},{2,10},{4,12},{6,14},{8,0},{10,2},{12,4},{14,6},{16,24},{18,... | collective-permute-start | bytes 3145736 | tf_op jit(solution)/shard_map/ppermute | solution.py:316
  133.8 26.5 %collective-permute-start.17 = (bf16[512,1024]{1,0:T(8,128)(2,1)}, bf16[512,1024]{1,0:T(8,128)(2,1)S(1)}, u32[]{:S(2)}, u32[]{:S(2)}) collective-permute-start(bf16[512,1024]{1,0:T(8,128)(2,1)} %collective-permute-done.14.refs_8_.refs_3_), channel_id=1, source_target_pairs={{0,4},{2,6},{4,0},{6,2},{8,12},{10,14},{12,8},{14,10},{16,20},{18,... | collective-permute-start | bytes 3145736 | tf_op jit(solution)/shard_map/ppermute | solution.py:316
  135.6 36.8 %collective-permute-start.38 = (bf16[1024,512]{1,0:T(8,128)(2,1)S(1)}, bf16[1024,512]{1,0:T(8,128)(2,1)S(1)}, u32[]{:S(2)}, u32[]{:S(2)}) collective-permute-start(bf16[1024,512]{1,0:T(8,128)(2,1)S(1)} %maximum_select_fusion.1), channel_id=1, source_target_pairs={{0,1},{1,0},{2,3},{3,2},{4,5},{5,4},{6,7},{7,6},{8,9},{9,8},{10,11... | collective-permute-start | bytes 3145736 | tf_op jit(solution)/shard_map/ppermute | solution.py:319
  145.6 37.5 %collective-permute-start.13 = (bf16[512,1024]{1,0:T(8,128)(2,1)}, bf16[512,1024]{1,0:T(8,128)(2,1)S(1)}, u32[]{:S(2)}, u32[]{:S(2)}) collective-permute-start(bf16[512,1024]{1,0:T(8,128)(2,1)} %collective-permute-done.12.refs_7_.refs_0_), channel_id=1, source_target_pairs={{0,4},{2,6},{4,0},{6,2},{8,12},{10,14},{12,8},{14,10},{16,20},{18,... | collective-permute-start | bytes 3145736 | tf_op jit(solution)/shard_map/ppermute | solution.py:316
  149.1 36.1 %collective-permute-start.39 = (bf16[1024,512]{1,0:T(8,128)(2,1)S(1)}, bf16[1024,512]{1,0:T(8,128)(2,1)S(1)}, u32[]{:S(2)}, u32[]{:S(2)}) collective-permute-start(bf16[1024,512]{1,0:T(8,128)(2,1)S(1)} %maximum_select_fusion.2), channel_id=1, source_target_pairs={{0,1},{1,0},{2,3},{3,2},{4,5},{5,4},{6,7},{7,6},{8,9},{9,8},{10,11... | collective-permute-start | bytes 3145736 | tf_op jit(solution)/shard_map/ppermute | solution.py:319
  169.9 58.2 %collective-permute-start.18 = (bf16[384,1024]{1,0:T(8,128)(2,1)S(1)}, bf16[384,1024]{1,0:T(8,128)(2,1)S(1)}, u32[]{:S(2)}, u32[]{:S(2)}) collective-permute-start(bf16[384,1024]{1,0:T(8,128)(2,1)S(1)} %slice.81), channel_id=1, source_target_pairs={{0,8},{2,10},{4,12},{6,14},{8,0},{10,2},{12,4},{14,6},{16,24},{18,... | collective-permute-start | bytes 2359304 | tf_op jit(solution)/shard_map/ppermute | solution.py:316
  183.1 97.4 %collective-permute-start.29 = (bf16[2048,512]{1,0:T(8,128)(2,1)}, bf16[2048,512]{1,0:T(8,128)(2,1)}, u32[]{:S(2)}, u32[]{:S(2)}) collective-permute-start(bf16[2048,512]{1,0:T(8,128)(2,1)} %maximum_select_fusion.w_ref), channel_id=1, source_target_pairs={{0,2},{2,0},{4,6},{6,4},{8,10},{10,8},{12,14},{14,12},{16,18},{18,... | collective-permute-start | bytes 6291464 | tf_op jit(solution)/shard_map/ppermute | solution.py:316
  183.1 47.9 %collective-permute-start.19 = (bf16[256,1024]{1,0:T(8,128)(2,1)S(1)}, bf16[256,1024]{1,0:T(8,128)(2,1)S(1)}, u32[]{:S(2)}, u32[]{:S(2)}) collective-permute-start(bf16[256,1024]{1,0:T(8,128)(2,1)S(1)} %get-tuple-element.42), channel_id=1, source_target_pairs={{0,4},{2,6},{4,0},{6,2},{8,12},{10,14},{12,8},{14,10},{16,20},{18,... | collective-permute-start | bytes 1572872 | tf_op jit(solution)/shard_map/ppermute | solution.py:316
  184.7 46.4 %collective-permute-start.20 = (bf16[256,1024]{1,0:T(8,128)(2,1)S(1)}, bf16[256,1024]{1,0:T(8,128)(2,1)S(1)}, u32[]{:S(2)}, u32[]{:S(2)}) collective-permute-start(bf16[256,1024]{1,0:T(8,128)(2,1)S(1)} %get-tuple-element.41), channel_id=1, source_target_pairs={{0,4},{2,6},{4,0},{6,2},{8,12},{10,14},{12,8},{14,10},{16,20},{18,... | collective-permute-start | bytes 1572872 | tf_op jit(solution)/shard_map/ppermute | solution.py:316
  185.2 40.0 %collective-permute-start.25 = (bf16[2,128,128]{2,1,0:T(8,128)(2,1)S(1)}, bf16[2,128,128]{2,1,0:T(8,128)(2,1)S(1)}, u32[]{:S(2)}, u32[]{:S(2)}) collective-permute-start(bf16[2,128,128]{2,1,0:T(8,128)(2,1)S(1)} %fusion.6), channel_id=1, source_target_pairs={{0,16},{2,18},{4,20},{6,22},{8,24},{10,26},{12,28},{14,30},{16,0},... | collective-permute-start | bytes 196616 | tf_op jit(solution)/shard_map/ppermute | solution.py:316
  225.2 87.2 %collective-permute-start.40 = (bf16[2048,512]{1,0:T(8,128)(2,1)}, bf16[2048,512]{1,0:T(8,128)(2,1)}, u32[]{:S(2)}, u32[]{:S(2)}) collective-permute-start(bf16[2048,512]{1,0:T(8,128)(2,1)} %bitcast.17), channel_id=1, source_target_pairs={{0,2},{2,0},{4,6},{6,4},{8,10},{10,8},{12,14},{14,12},{16,18},{18,... | collective-permute-start | bytes 6291464 | tf_op jit(solution)/shard_map/ppermute | solution.py:316
  237.0 41.6 %collective-permute-start.30 = (bf16[2,2,256,512]{3,2,1,0:T(8,128)(2,1)}, bf16[2,2,256,512]{3,2,1,0:T(8,128)(2,1)}, u32[]{:S(2)}, u32[]{:S(2)}) collective-permute-start(bf16[2,2,256,512]{3,2,1,0:T(8,128)(2,1)} %get-tuple-element.35), channel_id=1, source_target_pairs={{0,2},{2,0},{4,6},{6,4},{8,10},{10,8},{12,14},{14,12},{16,18},{18,... | collective-permute-start | bytes 3145736 | tf_op jit(solution)/shard_map/ppermute | solution.py:316
  253.9 26.6 %collective-permute-start.32 = (bf16[2,1,256,512]{3,2,1,0:T(8,128)(2,1)S(1)}, bf16[2,1,256,512]{3,2,1,0:T(8,128)(2,1)S(1)}, u32[]{:S(2)}, u32[]{:S(2)}) collective-permute-start(bf16[2,1,256,512]{3,2,1,0:T(8,128)(2,1)S(1)} %get-tuple-element.38), channel_id=1, source_target_pairs={{0,2},{2,0},{4,6},{6,4},{8,10},{10,8},{12,14},{14,12},{16,18},{18,... | collective-permute-start | bytes 1572872 | tf_op jit(solution)/shard_map/ppermute | solution.py:316
  279.9 28.1 %collective-permute-start.31 = (bf16[2,256,512]{2,1,0:T(8,128)(2,1)S(1)}, bf16[2,256,512]{2,1,0:T(8,128)(2,1)S(1)}, u32[]{:S(2)}, u32[]{:S(2)}) collective-permute-start(bf16[2,256,512]{2,1,0:T(8,128)(2,1)S(1)} %fusion), channel_id=1, source_target_pairs={{0,1},{1,0},{2,3},{3,2},{4,5},{5,4},{6,7},{7,6},{8,9},{9,8},{10,11... | collective-permute-start | bytes 1572872 | tf_op jit(solution)/shard_map/ppermute | solution.py:319
  287.0 27.6 %collective-permute-start.35 = (bf16[256,512]{1,0:T(8,128)(2,1)S(1)}, bf16[256,512]{1,0:T(8,128)(2,1)S(1)}, u32[]{:S(2)}, u32[]{:S(2)}) collective-permute-start(bf16[256,512]{1,0:T(8,128)(2,1)S(1)} %get-tuple-element.32.g_ref), channel_id=1, source_target_pairs={{0,1},{1,0},{2,3},{3,2},{4,5},{5,4},{6,7},{7,6},{8,9},{9,8},{10,11... | collective-permute-start | bytes 786440 | tf_op jit(solution)/shard_map/ppermute | solution.py:319
  (33 other events, 694.9 us)
